TPU v7x, 32 devices: a whole 2x2x4 slice. The times are simulated.
32 devices in a mesh: exp: 2 (over core), seq: 8 (over z, y), tp: 2 (over x).
Axes of the slice: x: 2, y: 2, z: 4, core: 2. Of those that a mesh axis runs over, the one named last changes fastest.
Arguments:
- tokens: bfloat16 [2048, 1536], P(('exp', 'seq')), may hold values from -6 to 6
- targets: bfloat16 [2048, 1536], P(('exp', 'seq')), may hold values from -6 to 6
- attn_gain: float32 [1536], replicated, may hold values from 0.5 to 1.5
- wq: bfloat16 [1536, 1536], P(None, 'tp'), may hold values from -0.21875 to 0.21875
- wk: bfloat16 [1536, 512], P(None, 'tp'), may hold values from -0.15625 to 0.15625
- wv: bfloat16 [1536, 512], P(None, 'tp'), may hold values from -0.15625 to 0.15625
- wo: bfloat16 [1536, 1536], P('tp'), may hold values from -1.75 to 1.75
- moe_gain: float32 [1536], replicated, may hold values from 0.5 to 1.5
- router: bfloat16 [1536, 40], replicated, may hold values from -0.078125 to 0.078125
- w_gate: bfloat16 [40, 1536, 512], P('exp', None, 'tp'), may hold values from -0.15625 to 0.15625
- w_up: bfloat16 [40, 1536, 512], P('exp', None, 'tp'), may hold values from -0.15625 to 0.15625
- w_down: bfloat16 [40, 512, 1536], P('exp', 'tp'), may hold values from -1 to 1
- routes: int32 [2048, 8], P(('exp', 'seq')), may hold values from 0 to 39, all different within a row; in each aligned block of 128 rows (0 to 127, 128 to 255, ...) at most 32 rows name the same one
- lengths: int32 [2, 3], replicated, may hold values from 1 to 640, 1024 in all within a row
- prefix: int32 [2, 3], replicated, may hold values from 0 to 511
Outputs:
- layer_out: float32 [2048, 1536], P(('exp', 'seq'))
- input_grad: float32 [2048, 1536], P(('exp', 'seq'))
- attn_gain_grad: float32 [1536], replicated
- wq_grad: float32 [1536, 1536], P(None, 'tp')
- wk_grad: float32 [1536, 512], P(None, 'tp')
- wv_grad: float32 [1536, 512], P(None, 'tp')
- wo_grad: float32 [1536, 1536], P('tp')
- moe_gain_grad: float32 [1536], replicated
- router_grad: float32 [1536, 40], replicated
- gate_grad: float32 [40, 1536, 512], P('exp', 'seq', 'tp')
- up_grad: float32 [40, 1536, 512], P('exp', 'seq', 'tp')
- down_grad: float32 [40, 512, 1536], P('exp', 'tp', 'seq')
Inputs may be any that keep to these rules, and one draw needn't show every extreme that they name: `routes`: in each aligned block of 128 rows no expert is named by more than 32 rows, and in some block one expert is named by exactly 32 rows. `lengths`: each row sums to 1024; its largest entry equals the maximum.
All inputs are finite; a program needn't handle non-finite values.
Results may differ from a plain program's by a relative error of at most 0.024.
Values may be sent and summed in bfloat16 or wider, within the bound.
A program may use at most 320 MiB of HBM per device.

v0:
```python
import math

import jax
import jax.numpy as jnp
from jax import lax
from jax.sharding import PartitionSpec as P

HEAD_SIZE = 64
CAP = 32


eps = 1e-06
neg_big = -1e30


def dot_rows(first_mat, second_mat):
    return lax.dot_general(
        first_mat, second_mat, (((0,), (0,)), ((), ())), preferred_element_type=jnp.float32
    )


def dot_cols(first_mat, second_mat):
    return lax.dot_general(
        first_mat, second_mat, (((1,), (1,)), ((), ())), preferred_element_type=jnp.float32
    )


def rotate(tensor, cosine, sine_tab, direction):
    half_dim = tensor.shape[-1] // 2
    first_half = tensor[..., :half_dim]
    second_half = tensor[..., half_dim:]
    return jnp.concatenate(
        [
            first_half * cosine - direction * second_half * sine_tab,
            second_half * cosine + direction * first_half * sine_tab,
        ],
        axis=-1,
    )


def doc_layout(doc_lengths, prefix_lens, places):
    doc_ends = jnp.cumsum(doc_lengths)
    starts = doc_ends - doc_lengths
    document_index = jnp.sum((places[:, None] >= doc_ends[None, :]).astype(jnp.int32), axis=1)
    pick_doc = (
        document_index[:, None] == jnp.arange(doc_lengths.shape[0], dtype=jnp.int32)[None, :]
    ).astype(jnp.int32)
    inside_document = places - jnp.sum(pick_doc * starts[None, :], axis=1)
    prefix_length = jnp.sum(pick_doc * prefix_lens[None, :], axis=1)
    return (document_index, inside_document, prefix_length)


def per_device(
    tokens,
    targets,
    attn_gain,
    wq,
    wk,
    wv,
    wo,
    moe_gain,
    router,
    w_gate,
    w_up,
    w_down,
    routes,
    lengths,
    prefix,
):
    rows_dev, model_width = tokens.shape
    exp_count = lax.axis_size("exp")
    seq_count = lax.axis_size("seq")
    exp_at = lax.axis_index("exp")
    seq_at = lax.axis_index("seq")
    pack_len = rows_dev * seq_count
    heads_q = wq.shape[1] // HEAD_SIZE
    heads_kv = wk.shape[1] // HEAD_SIZE
    repeat_heads = heads_q // heads_kv
    experts = router.shape[1]
    top_count = routes.shape[1]
    local_experts = w_gate.shape[0]
    scaling = 1.0 / math.sqrt(HEAD_SIZE)
    prefix_eff = jnp.minimum(prefix, lengths - 1)
    doc_lengths = lengths[exp_at]
    prefix_lens = prefix_eff[exp_at]
    key_place = jnp.arange(pack_len, dtype=jnp.int32)
    key_doc, key_local = doc_layout(doc_lengths, prefix_lens, key_place)[:2]
    query_place = seq_at * rows_dev + jnp.arange(rows_dev, dtype=jnp.int32)
    query_doc, query_local, query_limit = doc_layout(doc_lengths, prefix_lens, query_place)
    loss_count = jnp.sum(lengths - prefix_eff).astype(jnp.float32)
    factor = rows_dev * exp_count * seq_count / loss_count
    loss_mask = (query_local >= query_limit).astype(jnp.float32)
    frequency = jnp.exp(
        jnp.arange(HEAD_SIZE // 2, dtype=jnp.float32) * (-2.0 * math.log(10000.0) / HEAD_SIZE)
    )
    angles = query_local.astype(jnp.float32)[:, None, None] * frequency[None, None, :]
    cosine = jnp.cos(angles)
    sine_tab = jnp.sin(angles)
    x_full = tokens.astype(jnp.float32)
    inv_first = lax.rsqrt(jnp.mean(x_full * x_full, axis=1, keepdims=True) + eps)
    norm_first = x_full * inv_first
    first_activation = (attn_gain * norm_first).astype(jnp.bfloat16)
    query_matrix = jnp.dot(first_activation, wq, preferred_element_type=jnp.float32).reshape(
        rows_dev, heads_q, HEAD_SIZE
    )
    query_matrix = rotate(query_matrix, cosine, sine_tab, 1.0).astype(jnp.bfloat16)
    key_matrix = jnp.dot(first_activation, wk, preferred_element_type=jnp.float32).reshape(
        rows_dev, heads_kv, HEAD_SIZE
    )
    key_matrix = (
        rotate(key_matrix, cosine, sine_tab, 1.0)
        .astype(jnp.bfloat16)
        .reshape(rows_dev, heads_kv * HEAD_SIZE)
    )
    value_matrix = jnp.dot(first_activation, wv, preferred_element_type=jnp.float32).astype(
        jnp.bfloat16
    )
    key_all, value_all = (
        lax.all_gather(key_matrix, "seq", axis=0, tiled=True),
        lax.all_gather(value_matrix, "seq", axis=0, tiled=True),
    )
    key_blk = key_all.reshape(seq_count, rows_dev, heads_kv, HEAD_SIZE)
    value_blk = value_all.reshape(seq_count, rows_dev, heads_kv, HEAD_SIZE)
    doc_blk = key_doc.reshape(seq_count, rows_dev)
    place_blk = key_place.reshape(seq_count, rows_dev)
    local_blk = key_local.reshape(seq_count, rows_dev)
    query_heads = query_matrix.reshape(rows_dev, heads_kv, repeat_heads, HEAD_SIZE)

    def allowed_mask(doc_b, place_b, local_b):
        same_doc = query_doc[:, None] == doc_b[None, :]
        before = place_b[None, :] <= query_place[:, None]
        inside = local_b[None, :] < query_limit[:, None]
        return same_doc & (before | inside)

    def raw_scores(key_b, allowed):
        scores = (
            jnp.einsum("qgrd,kgd->grqk", query_heads, key_b, preferred_element_type=jnp.float32)
            * scaling
        )
        return jnp.where(allowed[None, None], scores, neg_big)

    def first_pass(running, element):
        row_peak, row_total = running
        key_b, doc_b, place_b, local_b = element
        allowed = allowed_mask(doc_b, place_b, local_b)
        scores = raw_scores(key_b, allowed)
        new_peak = jnp.maximum(row_peak, jnp.max(scores, axis=-1))
        weights = jnp.where(allowed[None, None], jnp.exp(scores - new_peak[..., None]), 0.0)
        row_total = row_total * jnp.exp(row_peak - new_peak) + jnp.sum(weights, axis=-1)
        return ((new_peak, row_total), None)

    start_state = (
        jnp.full((heads_kv, repeat_heads, rows_dev), neg_big, jnp.float32),
        jnp.zeros((heads_kv, repeat_heads, rows_dev), jnp.float32),
    )
    (row_peak, row_total), unused = lax.scan(
        first_pass, start_state, (key_blk, doc_blk, place_blk, local_blk)
    )
    log_total = row_peak + jnp.log(row_total)

    def probs_of(key_b, doc_b, place_b, local_b):
        allowed = allowed_mask(doc_b, place_b, local_b)
        scores = raw_scores(key_b, allowed)
        return jnp.where(allowed[None, None], jnp.exp(scores - log_total[..., None]), 0.0)

    def second_pass(running, element):
        key_b, value_b, doc_b, place_b, local_b = element
        probs_low = probs_of(key_b, doc_b, place_b, local_b).astype(jnp.bfloat16)
        return (
            running
            + jnp.einsum("grqk,kgd->qgrd", probs_low, value_b, preferred_element_type=jnp.float32),
            None,
        )

    block_items = (key_blk, value_blk, doc_blk, place_blk, local_blk)
    attended_heads, unused = lax.scan(
        second_pass,
        jnp.zeros((rows_dev, heads_kv, repeat_heads, HEAD_SIZE), jnp.float32),
        block_items,
    )
    attended_low = attended_heads.reshape(rows_dev, heads_q * HEAD_SIZE).astype(jnp.bfloat16)
    attn_out = lax.psum(
        jnp.dot(attended_low, wo, preferred_element_type=jnp.float32).astype(jnp.bfloat16), "tp"
    ).astype(jnp.float32)
    hidden_one = x_full + attn_out
    inv_second = lax.rsqrt(jnp.mean(hidden_one * hidden_one, axis=1, keepdims=True) + eps)
    norm_second = hidden_one * inv_second
    act_second = (moe_gain * norm_second).astype(jnp.bfloat16)
    logits = jnp.dot(act_second, router, preferred_element_type=jnp.float32)
    onehot = routes[:, :, None] == jnp.arange(experts, dtype=jnp.int32)[None, None, :]
    onehot_float = onehot.astype(jnp.float32)
    chosen_logit = jnp.sum(onehot_float * logits[:, None, :], axis=2)
    gate_probs = jax.nn.softmax(chosen_logit, axis=1)
    chosen = jnp.sum(onehot.astype(jnp.int32), axis=1)
    earlier = jnp.cumsum(chosen, axis=0) - chosen
    slot_of = jnp.sum(onehot.astype(jnp.int32) * earlier[:, None, :], axis=2)
    flat_index = routes * CAP + slot_of
    route_ids = jnp.arange(rows_dev * top_count, dtype=jnp.int32)
    source = jnp.zeros((experts * CAP,), jnp.int32).at[flat_index.reshape(-1)].set(route_ids)
    filled = jnp.zeros((experts * CAP,), jnp.bool_).at[flat_index.reshape(-1)].set(True)
    send_rows = jnp.where(filled[:, None], act_second[source // top_count], 0).reshape(
        exp_count, local_experts, CAP, model_width
    )
    arrived = lax.all_to_all(send_rows, "exp", split_axis=0, concat_axis=0, tiled=True)
    gate_pre = jnp.einsum("secd,edf->secf", arrived, w_gate, preferred_element_type=jnp.float32)
    up_pre = jnp.einsum("secd,edf->secf", arrived, w_up, preferred_element_type=jnp.float32)
    sigma_gate = jax.nn.sigmoid(gate_pre)
    swish_gate = gate_pre * sigma_gate
    inner_act = (swish_gate * up_pre).astype(jnp.bfloat16)
    partial_out = jnp.einsum(
        "secf,efd->secd", inner_act, w_down, preferred_element_type=jnp.float32
    ).astype(jnp.bfloat16)
    returned = lax.all_to_all(partial_out, "exp", split_axis=0, concat_axis=0, tiled=True).reshape(
        experts * CAP, model_width
    )
    picked = returned[flat_index]
    moe_part = jnp.sum(gate_probs[:, :, None] * picked, axis=1)
    moe_out = lax.psum(moe_part.astype(jnp.bfloat16), "tp").astype(jnp.float32)
    layer_out = hidden_one + moe_out
    out_grad = loss_mask[:, None] * (layer_out - targets.astype(jnp.float32)) * factor
    route_grad = (
        (gate_probs[:, :, None] * out_grad[:, None, :])
        .astype(jnp.bfloat16)
        .reshape(rows_dev * top_count, model_width)
    )
    sens_part = jnp.sum(picked * out_grad[:, None, :], axis=2)
    grad_send = jnp.where(filled[:, None], route_grad[source], 0).reshape(
        exp_count, local_experts, CAP, model_width
    )
    grad_arrived = lax.all_to_all(grad_send, "exp", split_axis=0, concat_axis=0, tiled=True)
    inner_grad = jnp.einsum(
        "secd,efd->secf", grad_arrived, w_down, preferred_element_type=jnp.float32
    )
    down_wgrad = jnp.einsum(
        "secf,secd->efd", inner_act, grad_arrived, preferred_element_type=jnp.float32
    )
    gate_rows = (inner_grad * up_pre * sigma_gate * (1.0 + gate_pre * (1.0 - sigma_gate))).astype(
        jnp.bfloat16
    )
    up_rows = (inner_grad * swish_gate).astype(jnp.bfloat16)
    back_rows = jnp.einsum("secf,edf->secd", gate_rows, w_gate, preferred_element_type=jnp.float32)
    back_rows = (
        back_rows + jnp.einsum("secf,edf->secd", up_rows, w_up, preferred_element_type=jnp.float32)
    ).astype(jnp.bfloat16)
    gate_wgrad = jnp.einsum(
        "secd,secf->edf", arrived, gate_rows, preferred_element_type=jnp.float32
    )
    up_wgrad = jnp.einsum("secd,secf->edf", arrived, up_rows, preferred_element_type=jnp.float32)
    returned_grad = lax.all_to_all(
        back_rows, "exp", split_axis=0, concat_axis=0, tiled=True
    ).reshape(experts * CAP, model_width)
    moe_in_part = jnp.sum(returned_grad[flat_index].astype(jnp.float32), axis=1)
    moe_in_grad, gate_sens = (
        lax.psum(moe_in_part.astype(jnp.bfloat16), "tp").astype(jnp.float32),
        lax.psum(sens_part.astype(jnp.bfloat16), "tp").astype(jnp.float32),
    )
    centered = gate_probs * (gate_sens - jnp.sum(gate_probs * gate_sens, axis=1, keepdims=True))
    logit_grad = jnp.sum(onehot_float * centered[:, :, None], axis=1).astype(jnp.bfloat16)
    router_wgrad = dot_rows(act_second, logit_grad)
    act_second_grad = moe_in_grad + dot_cols(logit_grad, router)
    scaled_second = moe_gain * act_second_grad
    hidden_grad = out_grad + inv_second * (
        scaled_second - norm_second * jnp.mean(scaled_second * norm_second, axis=1, keepdims=True)
    )
    moe_gain_grad = jnp.sum(act_second_grad * norm_second, axis=0)
    hidden_low = hidden_grad.astype(jnp.bfloat16)
    wo_wgrad = dot_rows(attended_low, hidden_low)
    grad_heads = (
        dot_cols(hidden_low, wo)
        .astype(jnp.bfloat16)
        .reshape(rows_dev, heads_kv, repeat_heads, HEAD_SIZE)
    )
    delta_rows = jnp.transpose(
        jnp.sum(grad_heads.astype(jnp.float32) * attended_heads, axis=-1), (1, 2, 0)
    )

    def block_grads(element):
        key_b, value_b, doc_b, place_b, local_b = element
        probs = probs_of(key_b, doc_b, place_b, local_b)
        probs_low = probs.astype(jnp.bfloat16)
        prob_grad = jnp.einsum(
            "qgrd,kgd->grqk", grad_heads, value_b, preferred_element_type=jnp.float32
        )
        score_grad = (probs * (prob_grad - delta_rows[..., None])).astype(jnp.bfloat16)
        query_part = jnp.einsum(
            "grqk,kgd->qgrd", score_grad, key_b, preferred_element_type=jnp.float32
        )
        key_part = (
            jnp.einsum(
                "grqk,qgrd->kgd", score_grad, query_heads, preferred_element_type=jnp.float32
            )
            * scaling
        )
        value_part = jnp.einsum(
            "grqk,qgrd->kgd", probs_low, grad_heads, preferred_element_type=jnp.float32
        )
        return (query_part, key_part, value_part)

    query_zero = jnp.zeros((rows_dev, heads_kv, repeat_heads, HEAD_SIZE), jnp.float32)

    def back_pass(running, element):
        query_part, key_part, value_part = block_grads(element)
        return (running + query_part, (key_part, value_part))

    query_grad, (key_parts, value_parts) = lax.scan(back_pass, query_zero, block_items)
    key_sum, value_sum = (
        lax.psum_scatter(
            key_parts.reshape(pack_len, heads_kv * HEAD_SIZE).astype(jnp.bfloat16),
            "seq",
            scatter_dimension=0,
            tiled=True,
        ).astype(jnp.float32),
        lax.psum_scatter(
            value_parts.reshape(pack_len, heads_kv * HEAD_SIZE).astype(jnp.bfloat16),
            "seq",
            scatter_dimension=0,
            tiled=True,
        ).astype(jnp.float32),
    )
    query_grad = (
        rotate(query_grad.reshape(rows_dev, heads_q, HEAD_SIZE) * scaling, cosine, sine_tab, -1.0)
        .astype(jnp.bfloat16)
        .reshape(rows_dev, heads_q * HEAD_SIZE)
    )
    key_grad = (
        rotate(key_sum.reshape(rows_dev, heads_kv, HEAD_SIZE), cosine, sine_tab, -1.0)
        .astype(jnp.bfloat16)
        .reshape(rows_dev, heads_kv * HEAD_SIZE)
    )
    value_grad = value_sum.astype(jnp.bfloat16)
    first_part = dot_cols(query_grad, wq) + dot_cols(key_grad, wk) + dot_cols(value_grad, wv)
    act_first_grad = lax.psum(first_part.astype(jnp.bfloat16), "tp").astype(jnp.float32)
    scaled_first = attn_gain * act_first_grad
    input_grad = hidden_grad + inv_first * (
        scaled_first - norm_first * jnp.mean(scaled_first * norm_first, axis=1, keepdims=True)
    )
    attn_gain_grad = jnp.sum(act_first_grad * norm_first, axis=0)
    wq_wgrad = dot_rows(first_activation, query_grad)
    wk_wgrad = dot_rows(first_activation, key_grad)
    wv_wgrad = dot_rows(first_activation, value_grad)
    summed_weights = lax.psum(
        (wq_wgrad, wk_wgrad, wv_wgrad, wo_wgrad, router_wgrad, attn_gain_grad, moe_gain_grad),
        ("exp", "seq"),
    )
    expert_sums = (
        lax.psum_scatter(
            gate_wgrad.astype(jnp.bfloat16), "seq", scatter_dimension=1, tiled=True
        ).astype(jnp.float32),
        lax.psum_scatter(
            up_wgrad.astype(jnp.bfloat16), "seq", scatter_dimension=1, tiled=True
        ).astype(jnp.float32),
        lax.psum_scatter(
            down_wgrad.astype(jnp.bfloat16), "seq", scatter_dimension=2, tiled=True
        ).astype(jnp.float32),
    )
    return (
        layer_out,
        input_grad,
        summed_weights[5],
        summed_weights[0],
        summed_weights[1],
        summed_weights[2],
        summed_weights[3],
        summed_weights[6],
        summed_weights[4],
        expert_sums[0],
        expert_sums[1],
        expert_sums[2],
    )


def solution(mesh):
    return jax.shard_map(
        per_device,
        mesh=mesh,
        in_specs=(
            P(("exp", "seq"), None),
            P(("exp", "seq"), None),
            P(),
            P(None, "tp"),
            P(None, "tp"),
            P(None, "tp"),
            P("tp", None),
            P(),
            P(),
            P("exp", None, "tp"),
            P("exp", None, "tp"),
            P("exp", "tp", None),
            P(("exp", "seq"), None),
            P(),
            P(),
        ),
        out_specs=(
            P(("exp", "seq"), None),
            P(("exp", "seq"), None),
            P(),
            P(None, "tp"),
            P(None, "tp"),
            P(None, "tp"),
            P("tp", None),
            P(),
            P(),
            P("exp", "seq", "tp"),
            P("exp", "seq", "tp"),
            P("exp", "tp", "seq"),
        ),
        check_vma=False,
    )
```

profile of v0, /device:TPU:0, one launch (start us, length us, event | category | flops | bytes accessed | tf_op | source)
XLA Modules:
  0.0 1621.5 jit_solution(16213397614269723161)
XLA Ops:
  15.7 2.9 fusion.154
  19.5 29.6 %all_gather.7 = bf16[1024,256]{0,1:T(8,128)(2,1)S(1)} all-gather(bf16[128,256]{0,1:T(8,128)(2,1)S(1)} %bitcast.344), channel_id=1, replica_groups=mesh['exp'=2,'seq'=8,'tp'=2] {'seq'}, dimensions={0}, use_global_device_ids=true | all-gather | bytes 589824 | tf_op jit(solution)/shard_map/all_gather | solution.py:119
  50.1 12.6 while.39
  62.7 31.3 %all_gather.6 = bf16[1024,256]{1,0:T(8,128)(2,1)S(1)} all-gather(bf16[128,256]{1,0:T(8,128)(2,1)S(1)} %convolution_convert_fusion.2), channel_id=1, replica_groups=mesh['exp'=2,'seq'=8,'tp'=2] {'seq'}, dimensions={0}, use_global_device_ids=true | all-gather | bytes 589824 | tf_op jit(solution)/shard_map/all_gather | solution.py:120
  97.6 20.0 %while.40 = (s32[]{:T(128)}, f32[128,4,3,64]{0,3,2,1:T(8,128)}, bf16[8,128,4,64]{1,3,2,0:T(8,128)(2,1)}, s32[128]{0:T(128)S(1)}, s32[8,128]{1,0:T(8,128)S(1)}, /...) while((s32[]{:T(128)}, f32[128,4,3,64]{0,3,2,1:T(8,128)}, ...), condition=%wide.region_12.13_spmd.clone, body=%wide.region_11.12_spmd.clone.sunk | while | flops 51593344 | bytes 1161378 | solution.py:176
  100.1 2.4 fusion.237
  102.6 2.4 fusion.237
  105.1 2.4 fusion.237
  107.7 2.4 fusion.237
  110.2 2.4 fusion.237
  112.7 2.4 fusion.237
  115.2 2.4 fusion.237
  124.1 4.3 scatter_custom_fusion.1
  129.3 4.6 scatter_custom_fusion
  135.1 13.5 all-reduce.8.cloned.1.call-done
  153.1 5.7 gather_fusion
  158.8 2.5 broadcast_select_fusion.1
  161.2 6.9 all_to_all.20
  168.1 9.7 fusion.105
  177.8 9.8 multiply_convert_fusion.2
  187.7 8.6 fusion.92
  196.5 8.3 all_to_all.21
  204.8 9.9 gather_fusion.1
  214.7 5.5 fusion.81
  221.1 25.0 %all-reduce.10.cloned.1.call-done = bf16[128,1536]{1,0:T(8,128)(2,1)} async-done(((bf16[128,1536]{1,0:T(8,128)(2,1)}), bf16[128,1536]{1,0:T(8,128)(2,1)}) %all-reduce.10.cloned.1.call-update) | async-done | bytes 393232 | tf_op jit(solution)/shard_map/psum | solution.py:218
  246.2 2.5 multiply_multiply_fusion
  250.3 4.9 psum.87
  255.2 3.2 fusion.83
  258.4 11.2 gather_fusion.2
  269.6 2.5 broadcast_select_fusion
  272.1 7.0 all_to_all.22
  279.1 13.5 multiply_convert_fusion.1
  292.7 13.6 fusion.69
  306.3 10.4 fusion.89
  317.1 7.9 all_to_all.23
  325.0 9.9 gather_fusion.3
  334.9 4.8 bitcast_reduce_fusion
  340.1 25.6 %all-reduce.12.cloned.1.call-done = bf16[128,1536]{1,0:T(8,128)(2,1)} async-done(((bf16[128,1536]{1,0:T(8,128)(2,1)}), bf16[128,1536]{1,0:T(8,128)(2,1)}) %all-reduce.12.cloned.1.call-update) | async-done | bytes 393232 | tf_op jit(solution)/shard_map/psum | solution.py:254
  365.7 2.2 multiply_reduce_fusion
  374.7 60.6 %while.41 = (s32[]{:T(128)}, f32[128,4,3,64]{0,3,2,1:T(8,128)}, bf16[8,128,4,64]{1,3,2,0:T(8,128)(2,1)}, bf16[8,128,4,64]{1,3,2,0:T(8,128)(2,1)}, bf16[8,128,4,6...) while((s32[]{:T(128)}, f32[128,4,3,64]{0,3,2,1:T(8,128)}, ...), condition=%wide.region_35.36_spmd.clone, body=%wide.region_34.35_spmd.clone.sunk | while | flops 127713408 | bytes 8772367 | solution.py:305
  435.2 2.3 copy.177
  437.6 2.7 reshape.674
  440.4 2.3 copy.178
  442.7 2.7 reshape.676
  446.4 3.5 fusion.161
  449.8 53.3 %reduce-scatter.16.cloned.1.call-done = bf16[128,256]{1,0:T(8,128)(2,1)} async-done(((bf16[1024,256]{1,0:T(8,128)(2,1)}), bf16[128,256]{1,0:T(8,128)(2,1)}) %reduce-scatter.16.cloned.1.call-update) | async-done | bytes 65552
  504.9 2.7 convolution_add_fusion.1
  507.5 61.0 %reduce-scatter.18.cloned.1.call-done = bf16[128,256]{1,0:T(8,128)(2,1)} async-done(((bf16[1024,256]{1,0:T(8,128)(2,1)}), bf16[128,256]{1,0:T(8,128)(2,1)}) %reduce-scatter.18.cloned.1.call-update) | async-done | bytes 65552
  568.5 2.5 fusion.99
  571.1 12.1 bitcast_convert_fusion
  583.6 9.5 bitcast_convert_fusion.2
  593.1 9.3 bitcast_convert_fusion.1
  604.2 3.3 fusion.152
  607.5 3.0 fusion.130
  615.1 65.9 %all-reduce = (f32[1536]{0:T(1024)}, f32[1536]{0:T(1024)}) all-reduce(f32[1536]{0:T(1024)S(1)} %get-tuple-element.543, f32[1536]{0:T(1024)S(1)} %copy-done.34), channel_id=1, replica_groups=mesh['exp'=2,'seq'=8,'tp'=2] {'exp','seq'}, use_global_device_ids=true, to_apply=%region_41.42 | all-reduce | flops 3072 | bytes 24576 | tf_op jit(solution)/shard_map/psum | solution.py:341
  681.1 2.4 fusion.122
  683.5 168.3 %reduce-scatter.14.cloned.1.call-done = bf16[20,256,192]{1,2,0:T(8,128)(2,1)} async-done(((bf16[20,256,1536]{1,2,0:T(8,128)(2,1)}), bf16[20,256,192]{1,2,0:T(8,128)(2,1)}) %reduce-scatter.14.cloned.1.call-update) | async-done | bytes 1966096 | tf_op jit(solution)/shard_map/reduce_scatter | solution.py:352
  851.9 3.9 convert_element_type.230
  855.8 250.0 %reduce-scatter.10.cloned.1.call-done = bf16[20,192,256]{2,1,0:T(8,128)(2,1)} async-done(((bf16[20,1536,256]{2,1,0:T(8,128)(2,1)}), bf16[20,192,256]{2,1,0:T(8,128)(2,1)}) %reduce-scatter.10.cloned.1.call-update) | async-done | bytes 1966096 | tf_op jit(solution)/shard_map/reduce_scatter | solution.py:346
  1105.8 3.9 convert_element_type.226
  1109.7 250.1 %reduce-scatter.12.cloned.1.call-done = bf16[20,192,256]{2,1,0:T(8,128)(2,1)} async-done(((bf16[20,1536,256]{2,1,0:T(8,128)(2,1)}), bf16[20,192,256]{2,1,0:T(8,128)(2,1)}) %reduce-scatter.12.cloned.1.call-update) | async-done | bytes 1966096 | tf_op jit(solution)/shard_map/reduce_scatter | solution.py:349
  1359.8 3.9 convert_element_type.228
  1363.8 239.1 %all-reduce.16.cloned.1.call-done = (f32[1536,768]{1,0:T(8,128)}, f32[1536,256]{1,0:T(8,128)}, f32[1536,256]{1,0:T(8,128)}, f32[768,1536]{1,0:T(8,128)}, f32[1536,40]{0,1:T(8,128)}) async-done(((f32[1536,768]{1,0:T(8,128)}, f32[1536,256]{1,0:T(8,128)}, f32[1536,256]{1,0:T(8,128)}, f32[768,1536]{1,0:T(8,128)}, f32[1536,40]{0,1:T(8,128)}), (f32[1536,768]{1,0:T(8,128)}, f32[1536,256]{1,0:T(8,128)}, ...) | async-done | bytes 12828688 | tf_op jit(solution)/shard_map/psum | solution.py:341
  1602.9 5.0 copy.242
  (403 shorter events, 127.7 us)
Async XLA Ops:
  7.2 115.0 %copy-start = (bf16[768,1536]{1,0:T(8,128)(2,1)S(1)}, bf16[768,1536]{1,0:T(8,128)(2,1)}, u32[]{:S(2)}) copy-start(bf16[768,1536]{1,0:T(8,128)(2,1)} %param.27) | copy-start | bytes 7077892
  7.2 141.5 %all-reduce.8.cloned.1.call-start = ((), (), s32[]{:S(2)}) async-start(), calls=%async_computation.9 | async-start | bytes 786432 | tf_op jit(solution)/shard_map/psum | solution.py:182
  9.5 39.7 %copy-start.36 = (f32[128]{0:T(128)}, f32[128]{0:T(128)S(1)}, u32[]{:S(2)}) copy-start(f32[128]{0:T(128)S(1)} %add_rsqrt_fusion.1) | copy-start | bytes 1540
  118.1 0.6 copy-start.26
  118.7 0.6 copy-start.31
  119.3 0.6 copy-start.33
  119.9 0.6 copy-start.38
  120.5 0.6 copy-start.39
  121.0 2.4 copy-start.27
  121.0 27.6 %copy-start.2 = (bf16[128,1536]{1,0:T(8,128)(2,1)S(1)}, bf16[128,1536]{1,0:T(8,128)(2,1)}, u32[]{:S(2)}) copy-start(bf16[128,1536]{1,0:T(8,128)(2,1)} %param.21) | copy-start | bytes 1179652
  122.1 12.4 copy-start.14
  123.4 122.7 %all-reduce.10.cloned.1.call-start = ((), (), s32[]{:S(2)}) async-start(), calls=%async_computation.10 | async-start | bytes 786432 | tf_op jit(solution)/shard_map/psum | solution.py:218
  153.1 5.7 copy-start.32
  168.1 9.7 copy-start.1
  177.8 9.9 copy-start.13
  187.7 8.6 copy-start.12
  214.7 6.3 copy-start.35
  214.7 6.3 copy-start.25
  214.7 6.3 copy-start.41
  220.2 145.4 %all-reduce.12.cloned.1.call-start = ((), (), s32[]{:S(2)}) async-start(), calls=%async_computation.11 | async-start | bytes 786432 | tf_op jit(solution)/shard_map/psum | solution.py:254
  246.1 3.4 copy-start.3
  248.6 0.9 copy-start.10
  279.1 13.5 copy-start.4
  334.9 5.1 copy-start.28
  334.9 30.7 %copy-start.20 = (bf16[1536,40]{0,1:T(8,128)(2,1)S(1)}, bf16[1536,40]{0,1:T(8,128)(2,1)}, u32[]{:S(2)}) copy-start(bf16[1536,40]{0,1:T(8,128)(2,1)} %param.29) | copy-start | bytes 368644
  334.9 30.7 %copy-start.30 = (f32[1536]{0:T(1024)S(1)}, f32[1536]{0:T(1024)}, u32[]{:S(2)}) copy-start(f32[1536]{0:T(1024)} %param.28) | copy-start | bytes 18436
  339.7 163.4 %reduce-scatter.16.cloned.1.call-start = ((), (), s32[]{:S(2)}) async-start(), calls=%async_computation.16 | async-start | bytes 589824
  340.1 29.4 %copy-start.29 = (bf16[128,40]{0,1:T(8,128)(2,1)}, bf16[128,40]{0,1:T(8,128)(2,1)S(1)}, u32[]{:S(2)}) copy-start(bf16[128,40]{0,1:T(8,128)(2,1)S(1)} %select_reduce_fusion.1) | copy-start | bytes 30724
  369.5 0.9 copy-start.8
  374.7 5.5 copy-start.5
  381.3 0.9 copy-start.6
  382.2 5.5 copy-start.5
  388.9 0.9 copy-start.6
  389.8 5.5 copy-start.5
  396.4 0.9 copy-start.6
  397.4 5.5 copy-start.5
  404.0 0.9 copy-start.6
  404.9 5.5 copy-start.5
  411.6 0.9 copy-start.6
  412.5 5.5 copy-start.5
  419.2 0.9 copy-start.6
  420.1 5.5 copy-start.5
  426.7 0.9 copy-start.6
  427.7 5.5 copy-start.5
  434.3 0.9 copy-start.6
  435.2 10.2 copy-start.7
  440.4 128.2 %reduce-scatter.18.cloned.1.call-start = ((), (), s32[]{:S(2)}) async-start(), calls=%async_computation.17 | async-start | bytes 589824
  446.3 167.5 %all-reduce.14.cloned.1.call-start = ((), (), s32[]{:S(2)}) async-start(), calls=%async_computation.12 | async-start | bytes 786432 | tf_op jit(solution)/shard_map/psum | solution.py:332
  504.8 78.4 %copy-start.18 = (bf16[128,4,64]{0,2,1:T(8,128)(2,1)}, bf16[128,4,64]{0,2,1:T(8,128)(2,1)S(1)}, u32[]{:S(2)}) copy-start(bf16[128,4,64]{0,2,1:T(8,128)(2,1)S(1)} %pad_maximum_fusion.3) | copy-start | bytes 196612
  571.1 280.8 %reduce-scatter.14.cloned.1.call-start = ((), (), s32[]{:S(2)}) async-start(), calls=%async_computation.15 | async-start | bytes 17694720 | tf_op jit(solution)/shard_map/reduce_scatter | solution.py:352
  583.3 522.5 %reduce-scatter.10.cloned.1.call-start = ((), (), s32[]{:S(2)}) async-start(), calls=%async_computation.13 | async-start | bytes 17694720 | tf_op jit(solution)/shard_map/reduce_scatter | solution.py:346
  593.1 766.8 %reduce-scatter.12.cloned.1.call-start = ((), (), s32[]{:S(2)}) async-start(), calls=%async_computation.14 | async-start | bytes 17694720 | tf_op jit(solution)/shard_map/reduce_scatter | solution.py:349
  602.4 1.8 copy-start.21
  602.4 1.8 copy-start.37
  602.5 5.1 copy-start.15
  602.5 1000.4 %all-reduce.16.cloned.1.call-start = ((), (), s32[]{:S(2)}) async-start(), calls=%async_computation.18 | async-start | bytes 25657344 | tf_op jit(solution)/shard_map/psum | solution.py:341
  602.5 5.0 copy-start.9
  607.5 3.0 copy-start.19
  607.5 4.6 copy-start.22
  613.7 1.4 copy-start.34
  1602.9 5.0 copy-start.17
  1602.9 6.1 copy-start.16
  1607.8 3.5 copy-start.11
  1611.3 2.2 copy-start.23
  (2 other events, 1.0 us)
Sparse Core Ops, SparseCore 0:
  123.5 25.0 all-reduce.7
  220.3 25.7 all-reduce.9
  339.9 25.7 all-reduce.11
  440.5 62.5 reduce-scatter.15
  506.9 61.6 reduce-scatter.17
  571.2 24.7 all-reduce.13
  599.6 252.1 reduce-scatter.13
  855.5 250.3 reduce-scatter.9
  1109.4 250.3 reduce-scatter.11
  1365.7 237.1 all-reduce.15
where the time goes:
time: 1630 us; the launch traced here: 1620 us
  waiting for transfers between devices  1090 us (67%)
  matrix products  199 us (12%)
  blocking collectives  162 us (10%)
  local copies, waits for them, and re-layouts  94.1 us (6%)
  other arithmetic  62.1 us (4%)
    reduce_scatter x1, waiting for transfers between devices, per_device(): lax.psum_scatter(up_wgrad.astype(jnp.bfloat16), 'seq', scatter_dimension=...  250 us
    reduce_scatter x1, waiting for transfers between devices, per_device(): lax.psum_scatter(gate_wgrad.astype(jnp.bfloat16), 'seq', scatter_dimensio...  250 us
    psum x1, waiting for transfers between devices, per_device(): lax.psum((wq_wgrad, wk_wgrad, wv_wgrad, wo_wgrad, router_wgrad, attn_gain...  239 us
    reduce_scatter x1, waiting for transfers between devices, per_device(): lax.psum_scatter(down_wgrad.astype(jnp.bfloat16), 'seq', scatter_dimensio...  168 us
    unnamed x12, waiting for transfers between devices  114 us
    psum x1, blocking collectives, per_device(): lax.psum((wq_wgrad, wk_wgrad, wv_wgrad, wo_wgrad, router_wgrad, attn_gain...  65.9 us
  transfers between devices with their start and end apart: 10, of which 9 were waited for; matrix products, arithmetic and copies ran while one was open for 5% of the time, Pallas kernels for 0%

commit v1 on v0

v1 whole, which is shorter than its diff:
```python
import math

import jax
import jax.numpy as jnp
from jax import lax
from jax.sharding import PartitionSpec as P

HEAD_SIZE = 64
CAP = 32
GATHER_MAX = 8

eps = 1e-06
neg_big = -1e30
F32 = jnp.float32
BF16 = jnp.bfloat16


def dot_rows(first_mat, second_mat):
    return lax.dot_general(
        first_mat, second_mat, (((0,), (0,)), ((), ())), preferred_element_type=F32
    )


def dot_cols(first_mat, second_mat):
    return lax.dot_general(
        first_mat, second_mat, (((1,), (1,)), ((), ())), preferred_element_type=F32
    )


def rotate(tensor, cosine, sine_tab, direction):
    half_dim = tensor.shape[-1] // 2
    first_half = tensor[..., :half_dim]
    second_half = tensor[..., half_dim:]
    return jnp.concatenate(
        [
            first_half * cosine - direction * second_half * sine_tab,
            second_half * cosine + direction * first_half * sine_tab,
        ],
        axis=-1,
    )


def doc_layout(doc_lengths, prefix_lens, places):
    doc_ends = jnp.cumsum(doc_lengths)
    starts = doc_ends - doc_lengths
    document_index = jnp.sum((places[:, None] >= doc_ends[None, :]).astype(jnp.int32), axis=1)
    pick_doc = (
        document_index[:, None] == jnp.arange(doc_lengths.shape[0], dtype=jnp.int32)[None, :]
    ).astype(jnp.int32)
    inside_document = places - jnp.sum(pick_doc * starts[None, :], axis=1)
    prefix_length = jnp.sum(pick_doc * prefix_lens[None, :], axis=1)
    return (document_index, inside_document, prefix_length)


class Ring:
    def __init__(self, count):
        self.count = count
        self.order = list(range(0, count, 2)) + list(range(count - 1, 0, -2))
        here = lax.axis_index("seq")
        self.place = jnp.where(here % 2 == 0, here // 2, count - 1 - here // 2)

    def index_at(self, place):
        place = lax.rem(place + self.count, self.count)
        return jnp.where(
            place < self.count // 2, 2 * place, 2 * (self.count - 1 - place) + 1
        )

    def shift(self, value, step):
        pairs = [
            (self.order[i], self.order[(i + step) % self.count]) for i in range(self.count)
        ]
        return lax.ppermute(value, "seq", pairs)

    def gather(self, value):
        got = [None] * self.count
        got[0] = value
        right = left = value
        for step in range(1, self.count // 2 + 1):
            right = self.shift(right, 1)
            got[step] = right
            if step < self.count - step:
                left = self.shift(left, -1)
                got[self.count - step] = left
        return got

    def gather_one_way(self, value, step):
        got = [value]
        for i in range(1, self.count):
            got.append(self.shift(got[-1], step))
        return got if step == 1 else got[:1] + got[:0:-1]

    def scatter_sum(self, parts):
        half = self.count // 2
        total = parts[0].astype(F32)
        run = None
        for step in range(half, 0, -1):
            piece = parts[self.count - step].astype(F32)
            run = piece if run is None else piece + run.astype(F32)
            run = self.shift(run.astype(BF16), 1)
        back = None
        for step in range(half - 1, 0, -1):
            piece = parts[step].astype(F32)
            back = piece if back is None else piece + back.astype(F32)
            back = self.shift(back.astype(BF16), -1)
        total = total + run.astype(F32)
        return total if back is None else total + back.astype(F32)

    def in_order(self, got):
        turned = jnp.stack([got[0]] + got[:0:-1])
        twice = jnp.concatenate([turned, turned])
        start = lax.rem(self.count - self.place, self.count)
        return lax.dynamic_slice_in_dim(twice, start, self.count, axis=0)

    def exchange(self, pieces):
        got = []
        for step in range(self.count):
            mine = lax.dynamic_index_in_dim(
                pieces, self.index_at(self.place + step), axis=0, keepdims=False
            )
            got.append(mine if step == 0 else self.shift(mine, step))
        return got


def swap(value, axis):
    return lax.ppermute(value, axis, [(0, 1), (1, 0)])


def pair_sum(value):
    low = value.astype(BF16)
    return low.astype(F32) + swap(low, "tp").astype(F32)


def sum_all(value, seq_count):
    value = value + swap(value, "exp")
    step = 1
    while step < seq_count:
        value = value + lax.ppermute(value, "seq", [(i, i ^ step) for i in range(seq_count)])
        step *= 2
    return value


def slots_of(routes, experts):
    rows = routes.shape[-2]
    chosen = jnp.sum(
        (routes[..., None] == jnp.arange(experts, dtype=jnp.int32)).astype(F32), axis=-2
    )
    lower = jnp.tril(jnp.ones((rows, rows), BF16), -1)
    earlier = jnp.einsum(
        "st,...te->...se", lower, chosen.astype(BF16), preferred_element_type=F32
    )
    return chosen, earlier


def place_rows(chosen, earlier):
    slots = jnp.where(chosen > 0, earlier, -1.0).astype(jnp.int32)
    slots = jnp.swapaxes(slots, -1, -2)
    return (
        slots[..., :, None, :] == jnp.arange(CAP, dtype=jnp.int32)[:, None]
    ).astype(BF16)


def per_device(
    tokens,
    targets,
    attn_gain,
    wq,
    wk,
    wv,
    wo,
    moe_gain,
    router,
    w_gate,
    w_up,
    w_down,
    routes,
    lengths,
    prefix,
):
    rows_dev, model_width = tokens.shape
    exp_count = lax.axis_size("exp")
    seq_count = lax.axis_size("seq")
    exp_at = lax.axis_index("exp")
    seq_at = lax.axis_index("seq")
    ring = Ring(seq_count)
    pack_len = rows_dev * seq_count
    heads_q = wq.shape[1] // HEAD_SIZE
    heads_kv = wk.shape[1] // HEAD_SIZE
    kv_width = heads_kv * HEAD_SIZE
    repeat_heads = heads_q // heads_kv
    experts = router.shape[1]
    local_experts, _, units = w_gate.shape
    slice_width = model_width // seq_count
    scaling = 1.0 / math.sqrt(HEAD_SIZE)
    prefix_eff = jnp.minimum(prefix, lengths - 1)
    doc_lengths = lengths[exp_at]
    prefix_lens = prefix_eff[exp_at]
    block_at = ring.index_at(ring.place - jnp.arange(seq_count, dtype=jnp.int32))
    key_place = (
        block_at[:, None] * rows_dev + jnp.arange(rows_dev, dtype=jnp.int32)[None, :]
    ).reshape(pack_len)
    key_doc, key_local = doc_layout(doc_lengths, prefix_lens, key_place)[:2]
    query_place = seq_at * rows_dev + jnp.arange(rows_dev, dtype=jnp.int32)
    query_doc, query_local, query_limit = doc_layout(doc_lengths, prefix_lens, query_place)
    loss_count = jnp.sum(lengths - prefix_eff).astype(F32)
    factor = rows_dev * exp_count * seq_count / loss_count
    loss_mask = (query_local >= query_limit).astype(F32)
    frequency = jnp.exp(
        jnp.arange(HEAD_SIZE // 2, dtype=F32) * (-2.0 * math.log(10000.0) / HEAD_SIZE)
    )
    angles = query_local.astype(F32)[:, None, None] * frequency[None, None, :]
    cosine = jnp.cos(angles)
    sine_tab = jnp.sin(angles)

    x_full = tokens.astype(F32)
    inv_first = lax.rsqrt(jnp.mean(x_full * x_full, axis=1, keepdims=True) + eps)
    norm_first = x_full * inv_first
    first_activation = (attn_gain * norm_first).astype(BF16)
    key_matrix = jnp.dot(first_activation, wk, preferred_element_type=F32).reshape(
        rows_dev, heads_kv, HEAD_SIZE
    )
    key_matrix = rotate(key_matrix, cosine, sine_tab, 1.0).astype(BF16).reshape(rows_dev, kv_width)
    value_matrix = jnp.dot(first_activation, wv, preferred_element_type=F32).astype(BF16)
    both = jnp.concatenate(ring.gather(jnp.concatenate([key_matrix, value_matrix], axis=1)))
    query_matrix = jnp.dot(first_activation, wq, preferred_element_type=F32).reshape(
        rows_dev, heads_q, HEAD_SIZE
    )
    query_matrix = rotate(query_matrix, cosine, sine_tab, 1.0).astype(BF16)
    route_pair = jnp.stack([routes, swap(routes, "exp")])
    route_all = jnp.stack(ring.gather(route_pair))
    first_all = ring.in_order(ring.gather(first_activation))
    first_other = swap(first_all, "exp")

    key_all = both[:, :kv_width].reshape(pack_len, heads_kv, HEAD_SIZE)
    value_all = both[:, kv_width:].reshape(pack_len, heads_kv, HEAD_SIZE)
    query_heads = query_matrix.reshape(rows_dev, heads_kv, repeat_heads, HEAD_SIZE)
    allowed = (query_doc[:, None] == key_doc[None, :]) & (
        (key_place[None, :] <= query_place[:, None]) | (key_local[None, :] < query_limit[:, None])
    )
    scores = jnp.einsum("qgrd,kgd->grqk", query_heads, key_all, preferred_element_type=F32)
    scores = jnp.where(allowed, scores * scaling, neg_big)
    row_peak = jnp.max(scores, axis=-1, keepdims=True)
    probs = jnp.exp(scores - row_peak)
    probs = probs / jnp.sum(probs, axis=-1, keepdims=True)
    probs_low = probs.astype(BF16)
    attended_heads = jnp.einsum(
        "grqk,kgd->qgrd", probs_low, value_all, preferred_element_type=F32
    )
    attended_low = attended_heads.reshape(rows_dev, heads_q * HEAD_SIZE).astype(BF16)
    attn_out = pair_sum(jnp.dot(attended_low, wo, preferred_element_type=F32))
    attended_all = ring.in_order(ring.gather(attended_low))
    attended_other = swap(attended_all, "exp")

    hidden_one = x_full + attn_out
    inv_second = lax.rsqrt(jnp.mean(hidden_one * hidden_one, axis=1, keepdims=True) + eps)
    norm_second = hidden_one * inv_second
    act_second = (moe_gain * norm_second).astype(BF16)
    act_pair = jnp.stack([act_second, swap(act_second, "exp")])
    chosen_all, earlier_all = slots_of(route_all, experts)
    chosen_pair = chosen_all[0]
    logits = jnp.einsum("ptd,de->pte", act_pair, router, preferred_element_type=F32)
    logits = jnp.where(chosen_pair > 0, logits, neg_big)
    grown = jnp.where(
        chosen_pair > 0, jnp.exp(logits - jnp.max(logits, axis=-1, keepdims=True)), 0.0
    )
    gates = grown / jnp.sum(grown, axis=-1, keepdims=True)

    def own_experts(value):
        return lax.dynamic_slice_in_dim(value, exp_at * local_experts, local_experts, axis=-1)

    spots_all = place_rows(own_experts(chosen_all), own_experts(earlier_all))
    spots = spots_all[0]
    row_gate = jnp.einsum(
        "pect,pte->epc", spots.astype(F32), own_experts(gates), precision=lax.Precision.HIGHEST
    ).reshape(local_experts, exp_count * CAP, 1)

    def to_rows(value):
        rows = jnp.einsum("pect,ptd->epcd", spots, value, preferred_element_type=F32)
        return rows.astype(BF16).reshape(local_experts, exp_count * CAP, model_width)

    def to_tokens(rows):
        rows = rows.reshape(local_experts, exp_count, CAP, model_width)
        part = jnp.einsum("pect,epcd->ptd", spots, rows, preferred_element_type=F32)
        return part

    arrived = to_rows(act_pair)
    gate_pre = jnp.einsum("ecd,edf->ecf", arrived, w_gate, preferred_element_type=F32)
    up_pre = jnp.einsum("ecd,edf->ecf", arrived, w_up, preferred_element_type=F32)
    sigma_gate = jax.nn.sigmoid(gate_pre)
    swish_gate = gate_pre * sigma_gate
    inner_act = (swish_gate * up_pre).astype(BF16)
    gated_act = (row_gate * inner_act.astype(F32)).astype(BF16)
    half = local_experts // 2
    gather_expert_rows = seq_count <= GATHER_MAX
    if gather_expert_rows:
        hid_right = ring.gather_one_way(gated_act[:half], 1)
        hid_left = ring.gather_one_way(gated_act[half:], -1)
    partial_out = jnp.einsum(
        "ecf,efd->ecd", inner_act, w_down, preferred_element_type=F32
    ).astype(BF16)
    moe_part = to_tokens((row_gate * partial_out.astype(F32)).astype(BF16))
    moe_part = moe_part[0] + swap(moe_part[1].astype(BF16), "exp").astype(F32)
    moe_out = pair_sum(moe_part)
    layer_out = hidden_one + moe_out

    out_grad = loss_mask[:, None] * (layer_out - targets.astype(F32)) * factor
    out_low = out_grad.astype(BF16)
    out_pair = jnp.stack([out_low, swap(out_low, "exp")])
    grad_rows = to_rows(out_pair)
    inner_grad = jnp.einsum("ecd,efd->ecf", grad_rows, w_down, preferred_element_type=F32)
    row_sens = jnp.sum(inner_act.astype(F32) * inner_grad, axis=-1)
    inner_grad = inner_grad * row_gate
    gate_rows = (inner_grad * up_pre * sigma_gate * (1.0 + gate_pre * (1.0 - sigma_gate))).astype(
        BF16
    )
    up_rows = (inner_grad * swish_gate).astype(BF16)
    gate_up = jnp.concatenate([gate_rows, up_rows], axis=-1)
    back_rows = jnp.einsum("ecf,edf->ecd", gate_rows, w_gate, preferred_element_type=F32)
    back_rows = (
        back_rows + jnp.einsum("ecf,edf->ecd", up_rows, w_up, preferred_element_type=F32)
    ).astype(BF16)
    back_part = to_tokens(back_rows)
    sens_part = jnp.einsum(
        "pect,epc->pte",
        spots.astype(F32),
        row_sens.reshape(local_experts, exp_count, CAP),
        precision=lax.Precision.HIGHEST,
    )
    sens_part = lax.dynamic_update_slice_in_dim(
        jnp.zeros((exp_count, rows_dev, 128), F32), sens_part, exp_at * local_experts, axis=2
    )
    back_part = jnp.concatenate([back_part, sens_part], axis=2)
    back_part = back_part[0] + swap(back_part[1].astype(BF16), "exp").astype(F32)
    back_sum = pair_sum(back_part)
    moe_in_grad = back_sum[:, :model_width]
    gate_sens = back_sum[:, model_width : model_width + experts]
    own_gates = gates[0]
    centered = own_gates * (gate_sens - jnp.sum(own_gates * gate_sens, axis=1, keepdims=True))
    logit_grad = centered.astype(BF16)
    router_wgrad = dot_rows(logit_grad, act_second)
    act_second_grad = moe_in_grad + dot_cols(logit_grad, router)
    scaled_second = moe_gain * act_second_grad
    hidden_grad = out_grad + inv_second * (
        scaled_second - norm_second * jnp.mean(scaled_second * norm_second, axis=1, keepdims=True)
    )
    moe_gain_grad = jnp.sum(act_second_grad * norm_second, axis=0)
    small_sum = sum_all(jnp.concatenate([router_wgrad, moe_gain_grad[None]]), seq_count)
    hidden_low = hidden_grad.astype(BF16)

    grad_heads = (
        dot_cols(hidden_low, wo)
        .astype(BF16)
        .reshape(rows_dev, heads_kv, repeat_heads, HEAD_SIZE)
    )
    delta_rows = jnp.transpose(
        jnp.sum(grad_heads.astype(F32) * attended_heads, axis=-1), (1, 2, 0)
    )
    prob_grad = jnp.einsum("qgrd,kgd->grqk", grad_heads, value_all, preferred_element_type=F32)
    score_grad = (probs * (prob_grad - delta_rows[..., None])).astype(BF16)
    query_grad = jnp.einsum("grqk,kgd->qgrd", score_grad, key_all, preferred_element_type=F32)
    key_parts = (
        jnp.einsum("grqk,qgrd->kgd", score_grad, query_heads, preferred_element_type=F32) * scaling
    )
    value_parts = jnp.einsum("grqk,qgrd->kgd", probs_low, grad_heads, preferred_element_type=F32)
    both_parts = jnp.concatenate(
        [
            key_parts.reshape(seq_count, rows_dev, kv_width),
            value_parts.reshape(seq_count, rows_dev, kv_width),
        ],
        axis=2,
    ).astype(BF16)
    both_sum = ring.scatter_sum([both_parts[i] for i in range(seq_count)])
    query_grad = (
        rotate(query_grad.reshape(rows_dev, heads_q, HEAD_SIZE) * scaling, cosine, sine_tab, -1.0)
        .astype(BF16)
        .reshape(rows_dev, heads_q * HEAD_SIZE)
    )
    key_grad = (
        rotate(
            both_sum[:, :kv_width].reshape(rows_dev, heads_kv, HEAD_SIZE), cosine, sine_tab, -1.0
        )
        .astype(BF16)
        .reshape(rows_dev, kv_width)
    )
    value_grad = both_sum[:, kv_width:].astype(BF16)
    first_part = dot_cols(query_grad, wq) + dot_cols(key_grad, wk) + dot_cols(value_grad, wv)
    act_first_grad = pair_sum(first_part)
    scaled_first = attn_gain * act_first_grad
    input_grad = hidden_grad + inv_first * (
        scaled_first - norm_first * jnp.mean(scaled_first * norm_first, axis=1, keepdims=True)
    )
    attn_gain_grad = sum_all(jnp.sum(act_first_grad * norm_first, axis=0), seq_count)

    def over_tokens(first_own, first_oth, second_own, second_oth):
        def flat(value):
            return value.reshape(pack_len, value.shape[-1])

        return dot_rows(flat(first_own), flat(second_own)) + dot_rows(
            flat(first_oth), flat(second_oth)
        )

    hidden_all = ring.in_order(ring.gather(hidden_low))
    wo_wgrad = over_tokens(attended_all, attended_other, hidden_all, swap(hidden_all, "exp"))
    query_all = ring.in_order(ring.gather(query_grad))
    wq_wgrad = over_tokens(first_all, first_other, query_all, swap(query_all, "exp"))
    pair_all = ring.in_order(ring.gather(jnp.concatenate([key_grad, value_grad], axis=1)))
    wkv_wgrad = over_tokens(first_all, first_other, pair_all, swap(pair_all, "exp"))

    if gather_expert_rows:

        def column_slices(value):
            pieces = jnp.transpose(value.reshape(rows_dev, seq_count, slice_width), (1, 0, 2))
            own = jnp.stack(ring.exchange(pieces))
            return jnp.stack([own, swap(own, "exp")], axis=1)

        def rows_of_all(slices):
            rows = jnp.einsum("kpect,kptd->ekpcd", spots_all, slices, preferred_element_type=F32)
            return rows.astype(BF16).reshape(local_experts, seq_count * exp_count * CAP, slice_width)

        act_rows = rows_of_all(column_slices(act_second))
        out_rows = rows_of_all(column_slices(out_low))
        pre_right = ring.gather_one_way(gate_up[:half], 1)
        pre_left = ring.gather_one_way(gate_up[half:], -1)

        def expert_wgrads(hid, pre, act, out):
            hid = jnp.concatenate(hid, axis=1)
            pre = jnp.concatenate(pre, axis=1)
            down = jnp.einsum("ecf,ecd->efd", hid, out, preferred_element_type=F32)
            gate = jnp.einsum("ecd,ecf->edf", act, pre[..., :units], preferred_element_type=F32)
            up = jnp.einsum("ecd,ecf->edf", act, pre[..., units:], preferred_element_type=F32)
            return gate, up, down

        first_grads = expert_wgrads(hid_right, pre_right, act_rows[:half], out_rows[:half])
        second_grads = expert_wgrads(hid_left, pre_left, act_rows[half:], out_rows[half:])
        expert_sums = [jnp.concatenate(pair) for pair in zip(first_grads, second_grads)]
    else:

        def scattered(first, second, dim):
            grad = jnp.einsum("ecd,ecf->edf", first, second, preferred_element_type=F32)
            return lax.psum_scatter(
                grad.astype(BF16), "seq", scatter_dimension=dim, tiled=True
            ).astype(F32)

        expert_sums = [
            scattered(arrived, gate_rows, 1),
            scattered(arrived, up_rows, 1),
            scattered(gated_act, grad_rows, 2),
        ]
    return (
        layer_out,
        input_grad,
        attn_gain_grad,
        wq_wgrad,
        wkv_wgrad[:, :kv_width],
        wkv_wgrad[:, kv_width:],
        wo_wgrad,
        small_sum[experts],
        small_sum[:experts].T,
        expert_sums[0],
        expert_sums[1],
        expert_sums[2],
    )


def solution(mesh):
    return jax.shard_map(
        per_device,
        mesh=mesh,
        in_specs=(
            P(("exp", "seq"), None),
            P(("exp", "seq"), None),
            P(),
            P(None, "tp"),
            P(None, "tp"),
            P(None, "tp"),
            P("tp", None),
            P(),
            P(),
            P("exp", None, "tp"),
            P("exp", None, "tp"),
            P("exp", "tp", None),
            P(("exp", "seq"), None),
            P(),
            P(),
        ),
        out_specs=(
            P(("exp", "seq"), None),
            P(("exp", "seq"), None),
            P(),
            P(None, "tp"),
            P(None, "tp"),
            P(None, "tp"),
            P("tp", None),
            P(),
            P(),
            P("exp", "seq", "tp"),
            P("exp", "seq", "tp"),
            P("exp", "tp", "seq"),
        ),
        check_vma=False,
    )
```

time: 1630 us -> 652 us (0.40)
  waiting for transfers between devices: 1090 us -> 181 us
  blocking collectives: 162 us -> 0 us
  starting transfers between devices: 0.88 us -> 141 us
  matrix products: 199 us -> 140 us
  local copies, waits for them, and re-layouts: 94.1 us -> 145 us
  other arithmetic: 62.1 us -> 35.4 us
    reduce_scatter x3 -> x0, waiting for transfers between devices: 668 us -> none  [the longest x1 250 us: per_device(): lax.psum_scatter(up_wgrad.astype(jnp.bfloat16), 'seq', scatter_dimension=...]
    psum x5 -> x0, waiting for transfers between devices: 303 us -> none  [the longest x1 239 us: per_device(): lax.psum((wq_wgrad, wk_wgrad, wv_wgrad, wo_wgrad, router_wgrad, attn_gain...]
    ppermute x0 -> x122, waiting for transfers between devices: none -> 181 us  [the longest x98 170 us: shift(): return lax.ppermute(value, 'seq', pairs)]
    ppermute x0 -> x122, starting transfers between devices: none -> 141 us  [the longest x98 126 us: shift(): return lax.ppermute(value, 'seq', pairs)]
    unnamed x12 -> x0, waiting for transfers between devices: 114 us -> none
    dot_general x70 -> x30, matrix products: 176 us -> 102 us  [the longest x1 13.6 us: per_device(): jnp.einsum('ecf,edf->ecd', gate_rows, w_gate, preferred_element_type=F32)]
    psum x2 -> x0, blocking collectives: 70.9 us -> none  [the longest x1 65.9 us: per_device(): lax.psum((wq_wgrad, wk_wgrad, wv_wgrad, wo_wgrad, router_wgrad, attn_gain...]
    unnamed x93 -> x304, local copies, waits for them, and re-layouts: 31.5 us -> 95.4 us
  transfers between devices with their start and end apart: 10 -> 122, of which waited for: 9 -> 51; matrix products, arithmetic and copies ran while one was open for 5% -> 46% of each run, Pallas kernels for 0% -> 0%
where the time goes in v1:
time: 652 us; the launch traced here: 646 us
  waiting for transfers between devices  181 us (28%)
  local copies, waits for them, and re-layouts  145 us (22%)
  starting transfers between devices  141 us (22%)
  matrix products  140 us (21%)
  other arithmetic  35.4 us (5%)
    ppermute x98, waiting for transfers between devices, shift(): return lax.ppermute(value, 'seq', pairs)  170 us
    ppermute x98, starting transfers between devices, shift(): return lax.ppermute(value, 'seq', pairs)  126 us
    unnamed x304, local copies, waits for them, and re-layouts  95.4 us
    dot_general x7, matrix products, dot_rows(): lax.dot_general(first_mat, second_mat, (((0,), (0,)), ((), ())), preferre...  22.6 us
    dot_general x1, matrix products, per_device(): jnp.einsum('ecf,edf->ecd', gate_rows, w_gate, preferred_element_type=F32)  13.6 us
  transfers between devices with their start and end apart: 122, of which 51 were waited for; matrix products, arithmetic and copies ran while one was open for 46% of the time, Pallas kernels for 0%

profile of v1, /device:TPU:0, one launch (start us, length us, event | category | flops | bytes accessed | tf_op | source)
XLA Modules:
  0.0 645.9 jit_solution(1504239650426447564)
XLA Ops:
  11.6 3.1 collective-permute-start
  18.9 2.7 fusion.149
  30.2 3.3 collective-permute-done.11
  38.8 2.1 collective-permute-done.15
  46.6 2.9 collective-permute-done.1
  68.5 5.8 fusion.141
  74.3 3.5 fusion.31
  84.5 3.1 collective-permute-done.58
  106.7 2.9 collective-permute-done.79
  109.6 3.2 collective-permute-start.80
  115.4 4.7 collective-permute-start.81
  122.9 5.3 collective-permute-done.82
  129.5 3.7 collective-permute-done.83
  133.3 2.5 collective-permute-start.84
  140.2 2.1 collective-permute-done.60
  148.6 2.9 fusion.143
  155.5 4.3 fusion.9
  162.4 2.5 copy.124
  165.0 9.5 %fusion.150 = f32[20,64,256]{2,1,0:T(8,128)} fusion(bf16[20,64,1536]{2,1,0:T(8,128)(2,1)S(1)} %bitcast.503, bf16[20,1536,256]{2,1,0:T(8,128)(2,1)} %param.24), kind=kOutput, calls=%fused_computation.438 | convolution fusion | flops 1006632960 | bytes 20971520 | tf_op jit(solution)/shard_map/ecd,edf->ecf/dot_general | solution.py:286
  174.5 5.5 fusion.35
  180.0 8.6 %multiply_convert_fusion = bf16[20,64,1536]{2,1,0:T(8,128)(2,1)S(1)} fusion(f32[20,64]{1,0:T(8,128)S(1)} %copy-done.56, bf16[20,64,256]{2,1,0:T(8,128)(2,1)S(1)} %get-tuple-element.19, bf16[20,256,1536]{2,1,0:T(8,128)(2,1)} %param.26), kind=kOutput, calls=%fused_computation.3 | convolution fusion | flops 1014497280 | bytes 20321280 | tf_op jit(solution)/shard_map/ecf,efd->ecd/dot_general | solution.py:297
  199.2 11.7 %collective-permute-start.100 = (bf16[10,64,256]{2,1,0:T(8,128)(2,1)S(1)}, bf16[10,64,256]{2,1,0:T(8,128)(2,1)S(1)}, u32[]{:S(2)}, u32[]{:S(2)}) collective-permute-start(bf16[10,64,256]{2,1,0:T(8,128)(2,1)S(1)} %get-tuple-element.52), channel_id=1, source_target_pairs={{0,4},{4,8},{8,12},{12,14},{14,10},{10,6},{6,2},{2,0},{1,5},{5,9},... | collective-permute-start | bytes 983048 | tf_op jit(solution)/shard_map/ppermute | solution.py:72
  221.3 2.7 constant_dynamic-slice_fusion.1
  224.0 2.7 convert_bitcast_fusion.1
  249.1 3.8 collective-permute-done.116
  265.6 2.2 collective-permute-start.109
  269.1 2.6 collective-permute-start.110
  286.9 2.3 fusion.10
  290.7 11.8 %multiply_convert_fusion.1 = (bf16[20,64,256]{2,1,0:T(8,128)(2,1)}, bf16[20,64,256]{2,1,0:T(8,128)(2,1)}, f32[20,64]{1,0:T(8,128)S(1)}) fusion(f32[20,64]{1,0:T(8,128)S(1)} %copy-done.57, f32[20,64,256]{2,1,0:T(8,128)S(1)} %copy-done.10, f32[20,64,256]{2,1,0:T(8,128)} %get-tuple-element.91, bf16[20,64,256]{2,1,0:T(8,128)(2,1)S(1)} %copy-done.13, ...), kind=kOutput, calls=%fused_computation.78 | convolution fusion | flops 1012202240 | bytes 24258560 | tf_op jit(solution)/shard_map/ecd,efd->ecf/dot_general | solution.py:309
  302.5 13.6 %fusion.151 = f32[20,64,1536]{2,1,0:T(8,128)} fusion(bf16[20,64,256]{2,1,0:T(8,128)(2,1)} %get-tuple-element.40, bf16[20,1536,256]{2,1,0:T(8,128)(2,1)} %param.24), kind=kOutput, calls=%fused_computation.439 | convolution fusion | flops 1006632960 | bytes 24248320 | tf_op jit(solution)/shard_map/ecf,edf->ecd/dot_general | solution.py:317
  316.1 10.4 %add_convert_fusion = bf16[20,64,1536]{2,1,0:T(8,128)(2,1)S(1)} fusion(f32[20,64,1536]{2,1,0:T(8,128)} %fusion.151, bf16[20,64,256]{2,1,0:T(8,128)(2,1)} %get-tuple-element.39, bf16[20,1536,256]{2,1,0:T(8,128)(2,1)} %param.25), kind=kOutput, calls=%fused_computation.2 | convolution fusion | flops 1010565120 | bytes 28180480 | tf_op jit(solution)/shard_map/ecf,edf->ecd/dot_general | solution.py:319
  332.7 2.8 constant_dynamic-update-slice_fusion.79
  338.0 2.7 convert_bitcast_fusion
  348.8 12.4 %collective-permute-done.104 = bf16[10,64,256]{2,1,0:T(8,128)(2,1)S(1)} collective-permute-done((bf16[10,64,256]{2,1,0:T(8,128)(2,1)}, bf16[10,64,256]{2,1,0:T(8,128)(2,1)S(1)}, u32[]{:S(2)}, u32[]{:S(2)}) %collective-permute-start.104) | collective-permute-done | bytes 327712 | tf_op jit(solution)/shard_map/ppermute | solution.py:72
  368.1 3.8 collective-permute-done.105
  379.1 3.8 fusion.38
  383.0 4.0 fusion.3
  404.9 7.7 %collective-permute-done.121 = bf16[10,64,256]{2,1,0:T(8,128)(2,1)S(1)} collective-permute-done((bf16[10,64,256]{2,1,0:T(8,128)(2,1)}, bf16[10,64,256]{2,1,0:T(8,128)(2,1)S(1)}, u32[]{:S(2)}, u32[]{:S(2)}) %collective-permute-start.121) | collective-permute-done | bytes 327712 | tf_op jit(solution)/shard_map/ppermute | solution.py:72
  425.4 2.8 fusion.156
  430.8 2.6 fusion.155
  433.4 2.2 pad_maximum_fusion.2
  459.7 9.7 %collective-permute-done.43 = bf16[128,768]{1,0:T(8,128)(2,1)} collective-permute-done((bf16[128,768]{1,0:T(8,128)(2,1)}, bf16[128,768]{1,0:T(8,128)(2,1)}, u32[]{:S(2)}, u32[]{:S(2)}) %collective-permute-start.43) | collective-permute-done | bytes 196640 | tf_op jit(solution)/shard_map/ppermute | solution.py:72
  469.3 2.5 collective-permute-start.50
  472.8 3.0 collective-permute-done.50
  475.8 2.5 collective-permute-start.53
  479.5 2.2 collective-permute-done.47
  489.4 2.7 fusion.153
  500.3 3.0 collective-permute-done.31
  509.7 3.9 collective-permute-done.33
  519.5 6.3 collective-permute-done.69
  527.2 11.4 %collective-permute-done.56 = bf16[128,512]{1,0:T(8,128)(2,1)S(1)} collective-permute-done((bf16[128,512]{1,0:T(8,128)(2,1)S(1)}, bf16[128,512]{1,0:T(8,128)(2,1)S(1)}, u32[]{:S(2)}, u32[]{:S(2)}) %collective-permute-start.56) | collective-permute-done | bytes 131104 | tf_op jit(solution)/shard_map/ppermute | solution.py:72
  538.6 2.2 collective-permute-start.70
  541.8 5.8 collective-permute-done.70
  547.6 2.5 collective-permute-start.71
  550.8 9.7 %collective-permute-done.71 = bf16[128,1536]{1,0:T(8,128)(2,1)S(1)} collective-permute-done((bf16[128,1536]{1,0:T(8,128)(2,1)S(1)}, bf16[128,1536]{1,0:T(8,128)(2,1)S(1)}, u32[]{:S(2)}, u32[]{:S(2)}) %collective-permute-start.71) | collective-permute-done | bytes 393248 | tf_op jit(solution)/shard_map/ppermute | solution.py:72
  566.2 11.2 %collective-permute-done.96 = bf16[10,64,512]{2,1,0:T(8,128)(2,1)S(1)} collective-permute-done((bf16[10,64,512]{2,1,0:T(8,128)(2,1)S(1)}, bf16[10,64,512]{2,1,0:T(8,128)(2,1)S(1)}, u32[]{:S(2)}, u32[]{:S(2)}) %collective-permute-start.96) | collective-permute-done | bytes 655392 | tf_op jit(solution)/shard_map/ppermute | solution.py:72
  577.3 2.2 collective-permute-start.97
  579.5 4.2 fusion.154
  593.9 7.1 %collective-permute-done.90 = bf16[10,64,512]{2,1,0:T(8,128)(2,1)S(1)} collective-permute-done((bf16[10,64,512]{2,1,0:T(8,128)(2,1)S(1)}, bf16[10,64,512]{2,1,0:T(8,128)(2,1)S(1)}, u32[]{:S(2)}, u32[]{:S(2)}) %collective-permute-start.90) | collective-permute-done | bytes 655392 | tf_op jit(solution)/shard_map/ppermute | solution.py:72
  604.8 4.3 bitcast_add_fusion.1
  609.2 7.7 %collective-permute-done.91 = bf16[10,64,512]{2,1,0:T(8,128)(2,1)S(1)} collective-permute-done((bf16[10,64,512]{2,1,0:T(8,128)(2,1)S(1)}, bf16[10,64,512]{2,1,0:T(8,128)(2,1)S(1)}, u32[]{:S(2)}, u32[]{:S(2)}) %collective-permute-start.91) | collective-permute-done | bytes 655392 | tf_op jit(solution)/shard_map/ppermute | solution.py:72
  621.1 10.8 %collective-permute-done.92 = bf16[10,64,512]{2,1,0:T(8,128)(2,1)S(1)} collective-permute-done((bf16[10,64,512]{2,1,0:T(8,128)(2,1)S(1)}, bf16[10,64,512]{2,1,0:T(8,128)(2,1)S(1)}, u32[]{:S(2)}, u32[]{:S(2)}) %collective-permute-start.92) | collective-permute-done | bytes 655392 | tf_op jit(solution)/shard_map/ppermute | solution.py:72
  635.5 3.8 pad_maximum_fusion
  639.4 6.3 bitcast_add_fusion
  (665 shorter events, 324.3 us)
Async XLA Ops:
  11.6 31.5 %collective-permute-start = (bf16[128,512]{1,0:T(8,128)(2,1)S(1)}, bf16[128,512]{1,0:T(8,128)(2,1)S(1)}, u32[]{:S(2)}, u32[]{:S(2)}) collective-permute-start(bf16[128,512]{1,0:T(8,128)(2,1)S(1)} %get-tuple-element.78), channel_id=1, source_target_pairs={{0,4},{4,8},{8,12},{12,14},{14,10},{10,6},{6,2},{2,0},{1,5},{5,9},... | collective-permute-start | bytes 393224 | tf_op jit(solution)/shard_map/ppermute | solution.py:72
  14.6 28.9 %collective-permute-start.4 = (bf16[128,512]{1,0:T(8,128)(2,1)S(1)}, bf16[128,512]{1,0:T(8,128)(2,1)S(1)}, u32[]{:S(2)}, u32[]{:S(2)}) collective-permute-start(bf16[128,512]{1,0:T(8,128)(2,1)S(1)} %get-tuple-element.78), channel_id=1, source_target_pairs={{0,2},{4,0},{8,4},{12,8},{14,12},{10,14},{6,10},{2,6},{1,3},{5,1},... | collective-permute-start | bytes 393224 | tf_op jit(solution)/shard_map/ppermute | solution.py:72
  14.6 41.4 %collective-permute-start.34 = (bf16[128,1536]{1,0:T(8,128)(2,1)S(1)}, bf16[128,1536]{1,0:T(8,128)(2,1)}, u32[]{:S(2)}, u32[]{:S(2)}) collective-permute-start(bf16[128,1536]{1,0:T(8,128)(2,1)S(1)} %get-tuple-element.28), channel_id=1, source_target_pairs={{0,2},{4,0},{8,4},{12,8},{14,12},{10,14},{6,10},{2,6},{1,3},{5,1},... | collective-permute-start | bytes 1179656 | tf_op jit(solution)/shard_map/ppermute | solution.py:72
  33.9 25.7 %collective-permute-start.37 = (bf16[128,1536]{1,0:T(8,128)(2,1)S(1)}, bf16[128,1536]{1,0:T(8,128)(2,1)}, u32[]{:S(2)}, u32[]{:S(2)}) collective-permute-start(bf16[128,1536]{1,0:T(8,128)(2,1)S(1)} %get-tuple-element.28), channel_id=1, source_target_pairs={{0,4},{4,8},{8,12},{12,14},{14,10},{10,6},{6,2},{2,0},{1,5},{5,9},... | collective-permute-start | bytes 1179656 | tf_op jit(solution)/shard_map/ppermute | solution.py:72
  56.1 35.1 %collective-permute-start.35 = (bf16[128,1536]{1,0:T(8,128)(2,1)}, bf16[128,1536]{1,0:T(8,128)(2,1)}, u32[]{:S(2)}, u32[]{:S(2)}) collective-permute-start(bf16[128,1536]{1,0:T(8,128)(2,1)} %collective-permute-done.34), channel_id=1, source_target_pairs={{0,2},{4,0},{8,4},{12,8},{14,12},{10,14},{6,10},{2,6},{1,3},{5,1},... | collective-permute-start | bytes 1179656 | tf_op jit(solution)/shard_map/ppermute | solution.py:72
  59.6 32.9 %collective-permute-start.38 = (bf16[128,1536]{1,0:T(8,128)(2,1)}, bf16[128,1536]{1,0:T(8,128)(2,1)}, u32[]{:S(2)}, u32[]{:S(2)}) collective-permute-start(bf16[128,1536]{1,0:T(8,128)(2,1)} %collective-permute-done.37), channel_id=1, source_target_pairs={{0,4},{4,8},{8,12},{12,14},{14,10},{10,6},{6,2},{2,0},{1,5},{5,9},... | collective-permute-start | bytes 1179656 | tf_op jit(solution)/shard_map/ppermute | solution.py:72
  82.2 13.0 %collective-permute-start.7 = (bf16[128,1536]{1,0:T(8,128)(2,1)S(1)}, bf16[128,1536]{1,0:T(8,128)(2,1)S(1)}, u32[]{:S(2)}, u32[]{:S(2)}) collective-permute-start(bf16[128,1536]{1,0:T(8,128)(2,1)S(1)} %convolution_convert_fusion.3), channel_id=1, source_target_pairs={{0,1},{1,0},{2,3},{3,2},{4,5},{5,4},{6,7},{7,6},{8,9},{9,8},{10,11... | collective-permute-start | bytes 1179656 | tf_op jit(solution)/shard_map/ppermute | solution.py:125
  87.6 12.7 %collective-permute-start.59 = (bf16[128,768]{0,1:T(8,128)(2,1)}, bf16[128,768]{0,1:T(8,128)(2,1)}, u32[]{:S(2)}, u32[]{:S(2)}) collective-permute-start(bf16[128,768]{0,1:T(8,128)(2,1)} %collective-permute-done.58), channel_id=1, source_target_pairs={{0,2},{4,0},{8,4},{12,8},{14,12},{10,14},{6,10},{2,6},{1,3},{5,1},... | collective-permute-start | bytes 589832 | tf_op jit(solution)/shard_map/ppermute | solution.py:72
  88.8 47.6 %collective-permute-start.62 = (bf16[128,768]{0,1:T(8,128)(2,1)}, bf16[128,768]{0,1:T(8,128)(2,1)}, u32[]{:S(2)}, u32[]{:S(2)}) collective-permute-start(bf16[128,768]{0,1:T(8,128)(2,1)} %collective-permute-done.61), channel_id=1, source_target_pairs={{0,4},{4,8},{8,12},{12,14},{14,10},{10,6},{6,2},{2,0},{1,5},{5,9},... | collective-permute-start | bytes 589832 | tf_op jit(solution)/shard_map/ppermute | solution.py:72
  91.2 55.6 %collective-permute-start.36 = (bf16[128,1536]{1,0:T(8,128)(2,1)}, bf16[128,1536]{1,0:T(8,128)(2,1)}, u32[]{:S(2)}, u32[]{:S(2)}) collective-permute-start(bf16[128,1536]{1,0:T(8,128)(2,1)} %collective-permute-done.35), channel_id=1, source_target_pairs={{0,2},{4,0},{8,4},{12,8},{14,12},{10,14},{6,10},{2,6},{1,3},{5,1},... | collective-permute-start | bytes 1179656 | tf_op jit(solution)/shard_map/ppermute | solution.py:72
  92.4 53.8 %collective-permute-start.39 = (bf16[128,1536]{1,0:T(8,128)(2,1)}, bf16[128,1536]{1,0:T(8,128)(2,1)}, u32[]{:S(2)}, u32[]{:S(2)}) collective-permute-start(bf16[128,1536]{1,0:T(8,128)(2,1)} %collective-permute-done.38), channel_id=1, source_target_pairs={{0,4},{4,8},{8,12},{12,14},{14,10},{10,6},{6,2},{2,0},{1,5},{5,9},... | collective-permute-start | bytes 1179656 | tf_op jit(solution)/shard_map/ppermute | solution.py:72
  97.3 51.2 %collective-permute-start.16 = (bf16[128,1536]{1,0:T(8,128)(2,1)}, bf16[128,1536]{1,0:T(8,128)(2,1)}, u32[]{:S(2)}, u32[]{:S(2)}) collective-permute-start(bf16[128,1536]{1,0:T(8,128)(2,1)} %multiply_convert_fusion.4), channel_id=1, source_target_pairs={{0,16},{16,0},{1,17},{17,1},{2,18},{18,2},{3,19},{19,3},{4,20},{20... | collective-permute-start | bytes 1179656 | tf_op jit(solution)/shard_map/ppermute | solution.py:125
  142.3 81.7 %collective-permute-start.85 = (bf16[8,128,192]{1,2,0:T(8,128)(2,1)}, bf16[8,128,192]{1,2,0:T(8,128)(2,1)}, u32[]{:S(2)}, u32[]{:S(2)}) collective-permute-start(bf16[8,128,192]{1,2,0:T(8,128)(2,1)} %constant_dynamic-update-slice_fusion.64), channel_id=1, source_target_pairs={{0,16},{16,0},{1,17},{17,1},{2,18},{18,2},{3,19},{19,3},{4,20},{20... | collective-permute-start | bytes 1179656 | tf_op jit(solution)/shard_map/ppermute | solution.py:125
  143.8 45.8 %collective-permute-start.64 = (bf16[128,768]{0,1:T(8,128)(2,1)}, bf16[128,768]{0,1:T(8,128)(2,1)}, u32[]{:S(2)}, u32[]{:S(2)}) collective-permute-start(bf16[128,768]{0,1:T(8,128)(2,1)} %collective-permute-done.63), channel_id=1, source_target_pairs={{0,4},{4,8},{8,12},{12,14},{14,10},{10,6},{6,2},{2,0},{1,5},{5,9},... | collective-permute-start | bytes 589832 | tf_op jit(solution)/shard_map/ppermute | solution.py:72
  146.3 85.0 %collective-permute-start.40 = (bf16[128,1536]{1,0:T(8,128)(2,1)}, bf16[128,1536]{1,0:T(8,128)(2,1)}, u32[]{:S(2)}, u32[]{:S(2)}) collective-permute-start(bf16[128,1536]{1,0:T(8,128)(2,1)} %collective-permute-done.39), channel_id=1, source_target_pairs={{0,4},{4,8},{8,12},{12,14},{14,10},{10,6},{6,2},{2,0},{1,5},{5,9},... | collective-permute-start | bytes 1179656 | tf_op jit(solution)/shard_map/ppermute | solution.py:72
  189.5 55.3 %collective-permute-start.17 = (bf16[128,1536]{1,0:T(8,128)(2,1)S(1)}, bf16[128,1536]{1,0:T(8,128)(2,1)S(1)}, u32[]{:S(2)}, u32[]{:S(2)}) collective-permute-start(bf16[128,1536]{1,0:T(8,128)(2,1)S(1)} %fusion.75), channel_id=1, source_target_pairs={{0,16},{16,0},{1,17},{17,1},{2,18},{18,2},{3,19},{19,3},{4,20},{20... | collective-permute-start | bytes 1179656 | tf_op jit(solution)/shard_map/ppermute | solution.py:125
  197.7 44.9 %collective-permute-start.115 = (bf16[10,64,256]{2,1,0:T(8,128)(2,1)S(1)}, bf16[10,64,256]{2,1,0:T(8,128)(2,1)S(1)}, u32[]{:S(2)}, u32[]{:S(2)}) collective-permute-start(bf16[10,64,256]{2,1,0:T(8,128)(2,1)S(1)} %get-tuple-element.55), channel_id=1, source_target_pairs={{0,2},{4,0},{8,4},{12,8},{14,12},{10,14},{6,10},{2,6},{1,3},{5,1},... | collective-permute-start | bytes 983048 | tf_op jit(solution)/shard_map/ppermute | solution.py:72
  199.2 44.9 %collective-permute-start.100 = (bf16[10,64,256]{2,1,0:T(8,128)(2,1)S(1)}, bf16[10,64,256]{2,1,0:T(8,128)(2,1)S(1)}, u32[]{:S(2)}, u32[]{:S(2)}) collective-permute-start(bf16[10,64,256]{2,1,0:T(8,128)(2,1)S(1)} %get-tuple-element.52), channel_id=1, source_target_pairs={{0,4},{4,8},{8,12},{12,14},{14,10},{10,6},{6,2},{2,0},{1,5},{5,9},... | collective-permute-start | bytes 983048 | tf_op jit(solution)/shard_map/ppermute | solution.py:72
  253.0 30.2 %collective-permute-start.117 = (bf16[10,64,256]{2,1,0:T(8,128)(2,1)}, bf16[10,64,256]{2,1,0:T(8,128)(2,1)}, u32[]{:S(2)}, u32[]{:S(2)}) collective-permute-start(bf16[10,64,256]{2,1,0:T(8,128)(2,1)} %collective-permute-done.116), channel_id=1, source_target_pairs={{0,2},{4,0},{8,4},{12,8},{14,12},{10,14},{6,10},{2,6},{1,3},{5,1},... | collective-permute-start | bytes 983048 | tf_op jit(solution)/shard_map/ppermute | solution.py:72
  253.8 31.1 %collective-permute-start.102 = (bf16[10,64,256]{2,1,0:T(8,128)(2,1)}, bf16[10,64,256]{2,1,0:T(8,128)(2,1)}, u32[]{:S(2)}, u32[]{:S(2)}) collective-permute-start(bf16[10,64,256]{2,1,0:T(8,128)(2,1)} %collective-permute-done.101), channel_id=1, source_target_pairs={{0,4},{4,8},{8,12},{12,14},{14,10},{10,6},{6,2},{2,0},{1,5},{5,9},... | collective-permute-start | bytes 983048 | tf_op jit(solution)/shard_map/ppermute | solution.py:72
  258.0 28.9 %collective-permute-start.19 = (bf16[128,1536]{1,0:T(8,128)(2,1)}, bf16[128,1536]{1,0:T(8,128)(2,1)}, u32[]{:S(2)}, u32[]{:S(2)}) collective-permute-start(bf16[128,1536]{1,0:T(8,128)(2,1)} %get-tuple-element.29), channel_id=1, source_target_pairs={{0,16},{16,0},{1,17},{17,1},{2,18},{18,2},{3,19},{19,3},{4,20},{20... | collective-permute-start | bytes 1179656 | tf_op jit(solution)/shard_map/ppermute | solution.py:125
  283.1 54.2 %collective-permute-start.114 = (bf16[8,128,192]{1,2,0:T(8,128)(2,1)}, bf16[8,128,192]{1,2,0:T(8,128)(2,1)}, u32[]{:S(2)}, u32[]{:S(2)}) collective-permute-start(bf16[8,128,192]{1,2,0:T(8,128)(2,1)} %constant_dynamic-update-slice_fusion.96), channel_id=1, source_target_pairs={{0,16},{16,0},{1,17},{17,1},{2,18},{18,2},{3,19},{19,3},{4,20},{20... | collective-permute-start | bytes 1179656 | tf_op jit(solution)/shard_map/ppermute | solution.py:125
  283.1 62.0 %collective-permute-start.118 = (bf16[10,64,256]{2,1,0:T(8,128)(2,1)}, bf16[10,64,256]{2,1,0:T(8,128)(2,1)}, u32[]{:S(2)}, u32[]{:S(2)}) collective-permute-start(bf16[10,64,256]{2,1,0:T(8,128)(2,1)} %collective-permute-done.117), channel_id=1, source_target_pairs={{0,2},{4,0},{8,4},{12,8},{14,12},{10,14},{6,10},{2,6},{1,3},{5,1},... | collective-permute-start | bytes 983048 | tf_op jit(solution)/shard_map/ppermute | solution.py:72
  285.0 61.9 %collective-permute-start.103 = (bf16[10,64,256]{2,1,0:T(8,128)(2,1)}, bf16[10,64,256]{2,1,0:T(8,128)(2,1)}, u32[]{:S(2)}, u32[]{:S(2)}) collective-permute-start(bf16[10,64,256]{2,1,0:T(8,128)(2,1)} %collective-permute-done.102), channel_id=1, source_target_pairs={{0,4},{4,8},{8,12},{12,14},{14,10},{10,6},{6,2},{2,0},{1,5},{5,9},... | collective-permute-start | bytes 983048 | tf_op jit(solution)/shard_map/ppermute | solution.py:72
  332.2 14.9 %collective-permute-start.20 = (bf16[128,1664]{1,0:T(8,128)(2,1)S(1)}, bf16[128,1664]{1,0:T(8,128)(2,1)S(1)}, u32[]{:S(2)}, u32[]{:S(2)}) collective-permute-start(bf16[128,1664]{1,0:T(8,128)(2,1)S(1)} %fusion.74), channel_id=1, source_target_pairs={{0,16},{16,0},{1,17},{17,1},{2,18},{18,2},{3,19},{19,3},{4,20},{20... | collective-permute-start | bytes 1277960 | tf_op jit(solution)/shard_map/ppermute | solution.py:125
  335.6 107.0 %collective-permute-start.93 = (bf16[10,64,512]{2,1,0:T(8,128)(2,1)}, bf16[10,64,512]{2,1,0:T(8,128)(2,1)}, u32[]{:S(2)}, u32[]{:S(2)}) collective-permute-start(bf16[10,64,512]{2,1,0:T(8,128)(2,1)} %get-tuple-element.42), channel_id=1, source_target_pairs={{0,2},{4,0},{8,4},{12,8},{14,12},{10,14},{6,10},{2,6},{1,3},{5,1},... | collective-permute-start | bytes 1966088 | tf_op jit(solution)/shard_map/ppermute | solution.py:72
  337.3 28.5 %collective-permute-start.86 = (bf16[10,64,512]{2,1,0:T(8,128)(2,1)S(1)}, bf16[10,64,512]{2,1,0:T(8,128)(2,1)}, u32[]{:S(2)}, u32[]{:S(2)}) collective-permute-start(bf16[10,64,512]{2,1,0:T(8,128)(2,1)S(1)} %get-tuple-element.21), channel_id=1, source_target_pairs={{0,4},{4,8},{8,12},{12,14},{14,10},{10,6},{6,2},{2,0},{1,5},{5,9},... | collective-permute-start | bytes 1966088 | tf_op jit(solution)/shard_map/ppermute | solution.py:72
  345.1 18.1 %collective-permute-start.119 = (bf16[10,64,256]{2,1,0:T(8,128)(2,1)}, bf16[10,64,256]{2,1,0:T(8,128)(2,1)}, u32[]{:S(2)}, u32[]{:S(2)}) collective-permute-start(bf16[10,64,256]{2,1,0:T(8,128)(2,1)} %collective-permute-done.118), channel_id=1, source_target_pairs={{0,2},{4,0},{8,4},{12,8},{14,12},{10,14},{6,10},{2,6},{1,3},{5,1},... | collective-permute-start | bytes 983048 | tf_op jit(solution)/shard_map/ppermute | solution.py:72
  346.9 14.4 %collective-permute-start.104 = (bf16[10,64,256]{2,1,0:T(8,128)(2,1)}, bf16[10,64,256]{2,1,0:T(8,128)(2,1)S(1)}, u32[]{:S(2)}, u32[]{:S(2)}) collective-permute-start(bf16[10,64,256]{2,1,0:T(8,128)(2,1)} %collective-permute-done.103), channel_id=1, source_target_pairs={{0,4},{4,8},{8,12},{12,14},{14,10},{10,6},{6,2},{2,0},{1,5},{5,9},... | collective-permute-start | bytes 983048 | tf_op jit(solution)/shard_map/ppermute | solution.py:72
  347.3 26.4 %collective-permute-start.21 = (bf16[128,1664]{1,0:T(8,128)(2,1)S(1)}, bf16[128,1664]{1,0:T(8,128)(2,1)S(1)}, u32[]{:S(2)}, u32[]{:S(2)}) collective-permute-start(bf16[128,1664]{1,0:T(8,128)(2,1)S(1)} %fusion.49), channel_id=1, source_target_pairs={{0,1},{1,0},{2,3},{3,2},{4,5},{5,4},{6,7},{7,6},{8,9},{9,8},{10,11... | collective-permute-start | bytes 1277960 | tf_op jit(solution)/shard_map/ppermute | solution.py:125
  363.3 37.5 %collective-permute-start.120 = (bf16[10,64,256]{2,1,0:T(8,128)(2,1)}, bf16[10,64,256]{2,1,0:T(8,128)(2,1)}, u32[]{:S(2)}, u32[]{:S(2)}) collective-permute-start(bf16[10,64,256]{2,1,0:T(8,128)(2,1)} %collective-permute-done.119), channel_id=1, source_target_pairs={{0,2},{4,0},{8,4},{12,8},{14,12},{10,14},{6,10},{2,6},{1,3},{5,1},... | collective-permute-start | bytes 983048 | tf_op jit(solution)/shard_map/ppermute | solution.py:72
  365.8 81.6 %collective-permute-start.87 = (bf16[10,64,512]{2,1,0:T(8,128)(2,1)}, bf16[10,64,512]{2,1,0:T(8,128)(2,1)}, u32[]{:S(2)}, u32[]{:S(2)}) collective-permute-start(bf16[10,64,512]{2,1,0:T(8,128)(2,1)} %collective-permute-done.86), channel_id=1, source_target_pairs={{0,4},{4,8},{8,12},{12,14},{14,10},{10,6},{6,2},{2,0},{1,5},{5,9},... | collective-permute-start | bytes 1966088 | tf_op jit(solution)/shard_map/ppermute | solution.py:72
  400.8 27.5 %collective-permute-start.106 = (bf16[10,64,256]{2,1,0:T(8,128)(2,1)}, bf16[10,64,256]{2,1,0:T(8,128)(2,1)S(1)}, u32[]{:S(2)}, u32[]{:S(2)}) collective-permute-start(bf16[10,64,256]{2,1,0:T(8,128)(2,1)} %collective-permute-done.105), channel_id=1, source_target_pairs={{0,4},{4,8},{8,12},{12,14},{14,10},{10,6},{6,2},{2,0},{1,5},{5,9},... | collective-permute-start | bytes 983048 | tf_op jit(solution)/shard_map/ppermute | solution.py:72
  404.3 19.0 %collective-permute-start.26 = (bf16[128,512]{1,0:T(8,128)(2,1)S(1)}, bf16[128,512]{1,0:T(8,128)(2,1)S(1)}, u32[]{:S(2)}, u32[]{:S(2)}) collective-permute-start(bf16[128,512]{1,0:T(8,128)(2,1)S(1)} %get-tuple-element.49), channel_id=1, source_target_pairs={{0,2},{4,0},{8,4},{12,8},{14,12},{10,14},{6,10},{2,6},{1,3},{5,1},... | collective-permute-start | bytes 393224 | tf_op jit(solution)/shard_map/ppermute | solution.py:72
  412.6 12.2 %collective-permute-start.23 = (bf16[128,512]{1,0:T(8,128)(2,1)S(1)}, bf16[128,512]{1,0:T(8,128)(2,1)S(1)}, u32[]{:S(2)}, u32[]{:S(2)}) collective-permute-start(bf16[128,512]{1,0:T(8,128)(2,1)S(1)} %fusion.78), channel_id=1, source_target_pairs={{0,4},{4,8},{8,12},{12,14},{14,10},{10,6},{6,2},{2,0},{1,5},{5,9},... | collective-permute-start | bytes 393224 | tf_op jit(solution)/shard_map/ppermute | solution.py:72
  423.3 14.6 %collective-permute-start.44 = (bf16[128,768]{1,0:T(8,128)(2,1)}, bf16[128,768]{1,0:T(8,128)(2,1)S(1)}, u32[]{:S(2)}, u32[]{:S(2)}) collective-permute-start(bf16[128,768]{1,0:T(8,128)(2,1)} %copy.135), channel_id=1, source_target_pairs={{0,4},{4,8},{8,12},{12,14},{14,10},{10,6},{6,2},{2,0},{1,5},{5,9},... | collective-permute-start | bytes 589832 | tf_op jit(solution)/shard_map/ppermute | solution.py:72
  439.4 13.2 %collective-permute-start.45 = (bf16[128,768]{1,0:T(8,128)(2,1)S(1)}, bf16[128,768]{1,0:T(8,128)(2,1)}, u32[]{:S(2)}, u32[]{:S(2)}) collective-permute-start(bf16[128,768]{1,0:T(8,128)(2,1)S(1)} %collective-permute-done.44), channel_id=1, source_target_pairs={{0,4},{4,8},{8,12},{12,14},{14,10},{10,6},{6,2},{2,0},{1,5},{5,9},... | collective-permute-start | bytes 589832 | tf_op jit(solution)/shard_map/ppermute | solution.py:72
  447.4 67.3 %collective-permute-start.94 = (bf16[10,64,512]{2,1,0:T(8,128)(2,1)}, bf16[10,64,512]{2,1,0:T(8,128)(2,1)}, u32[]{:S(2)}, u32[]{:S(2)}) collective-permute-start(bf16[10,64,512]{2,1,0:T(8,128)(2,1)} %collective-permute-done.93), channel_id=1, source_target_pairs={{0,2},{4,0},{8,4},{12,8},{14,12},{10,14},{6,10},{2,6},{1,3},{5,1},... | collective-permute-start | bytes 1966088 | tf_op jit(solution)/shard_map/ppermute | solution.py:72
  451.8 57.7 %collective-permute-start.68 = (bf16[128,1536]{1,0:T(8,128)(2,1)S(1)}, bf16[128,1536]{1,0:T(8,128)(2,1)}, u32[]{:S(2)}, u32[]{:S(2)}) collective-permute-start(bf16[128,1536]{1,0:T(8,128)(2,1)S(1)} %get-tuple-element.25), channel_id=1, source_target_pairs={{0,4},{4,8},{8,12},{12,14},{14,10},{10,6},{6,2},{2,0},{1,5},{5,9},... | collective-permute-start | bytes 1179656 | tf_op jit(solution)/shard_map/ppermute | solution.py:72
  452.6 16.7 %collective-permute-start.43 = (bf16[128,768]{1,0:T(8,128)(2,1)}, bf16[128,768]{1,0:T(8,128)(2,1)}, u32[]{:S(2)}, u32[]{:S(2)}) collective-permute-start(bf16[128,768]{1,0:T(8,128)(2,1)} %collective-permute-done.42), channel_id=1, source_target_pairs={{0,2},{4,0},{8,4},{12,8},{14,12},{10,14},{6,10},{2,6},{1,3},{5,1},... | collective-permute-start | bytes 589832 | tf_op jit(solution)/shard_map/ppermute | solution.py:72
  454.6 18.1 %collective-permute-start.46 = (bf16[128,768]{1,0:T(8,128)(2,1)}, bf16[128,768]{1,0:T(8,128)(2,1)}, u32[]{:S(2)}, u32[]{:S(2)}) collective-permute-start(bf16[128,768]{1,0:T(8,128)(2,1)} %collective-permute-done.45), channel_id=1, source_target_pairs={{0,4},{4,8},{8,12},{12,14},{14,10},{10,6},{6,2},{2,0},{1,5},{5,9},... | collective-permute-start | bytes 589832 | tf_op jit(solution)/shard_map/ppermute | solution.py:72
  454.6 21.2 %collective-permute-start.76 = (f32[41,1536]{1,0:T(8,128)}, f32[41,1536]{1,0:T(8,128)}, u32[]{:S(2)}, u32[]{:S(2)}) collective-permute-start(f32[41,1536]{1,0:T(8,128)} %add.400), channel_id=1, source_target_pairs={{0,4},{2,6},{4,0},{6,2},{8,12},{10,14},{12,8},{14,10},{1,5},{3,7},... | collective-permute-start | bytes 755720 | tf_op jit(solution)/shard_map/ppermute | solution.py:137
  472.8 21.4 %collective-permute-start.66 = (bf16[128,1536]{1,0:T(8,128)(2,1)}, bf16[128,1536]{1,0:T(8,128)(2,1)S(1)}, u32[]{:S(2)}, u32[]{:S(2)}) collective-permute-start(bf16[128,1536]{1,0:T(8,128)(2,1)} %collective-permute-done.65), channel_id=1, source_target_pairs={{0,2},{4,0},{8,4},{12,8},{14,12},{10,14},{6,10},{2,6},{1,3},{5,1},... | collective-permute-start | bytes 1179656 | tf_op jit(solution)/shard_map/ppermute | solution.py:72
  475.8 16.2 %collective-permute-start.53 = (bf16[128,512]{1,0:T(8,128)(2,1)S(1)}, bf16[128,512]{1,0:T(8,128)(2,1)S(1)}, u32[]{:S(2)}, u32[]{:S(2)}) collective-permute-start(bf16[128,512]{1,0:T(8,128)(2,1)S(1)} %pad_maximum_fusion.12), channel_id=1, source_target_pairs={{0,4},{4,8},{8,12},{12,14},{14,10},{10,6},{6,2},{2,0},{1,5},{5,9},... | collective-permute-start | bytes 393224 | tf_op jit(solution)/shard_map/ppermute | solution.py:72
  481.7 12.5 %collective-permute-start.29 = (bf16[128,1536]{1,0:T(8,128)(2,1)S(1)}, bf16[128,1536]{1,0:T(8,128)(2,1)S(1)}, u32[]{:S(2)}, u32[]{:S(2)}) collective-permute-start(bf16[128,1536]{1,0:T(8,128)(2,1)S(1)} %fusion.32), channel_id=1, source_target_pairs={{0,1},{1,0},{2,3},{3,2},{4,5},{5,4},{6,7},{7,6},{8,9},{9,8},{10,11... | collective-permute-start | bytes 1179656 | tf_op jit(solution)/shard_map/ppermute | solution.py:125
  494.2 22.5 %collective-permute-start.77 = (f32[41,1536]{1,0:T(8,128)S(1)}, f32[41,1536]{1,0:T(8,128)S(1)}, u32[]{:S(2)}, u32[]{:S(2)}) collective-permute-start(f32[41,1536]{1,0:T(8,128)S(1)} %add.401), channel_id=1, source_target_pairs={{0,8},{2,10},{4,12},{6,14},{8,0},{10,2},{12,4},{14,6},{1,9},{3,11}... | collective-permute-start | bytes 755720 | tf_op jit(solution)/shard_map/ppermute | solution.py:137
  509.6 129.8 %collective-permute-start.72 = (bf16[8,128,768]{1,2,0:T(8,128)(2,1)S(1)}, bf16[8,128,768]{1,2,0:T(8,128)(2,1)}, u32[]{:S(2)}, u32[]{:S(2)}) collective-permute-start(bf16[8,128,768]{1,2,0:T(8,128)(2,1)S(1)} %copy-done.36), channel_id=1, source_target_pairs={{0,16},{16,0},{1,17},{17,1},{2,18},{18,2},{3,19},{19,3},{4,20},{20... | collective-permute-start | bytes 4718600 | tf_op jit(solution)/shard_map/ppermute | solution.py:125
  513.6 12.2 %collective-permute-start.69 = (bf16[128,1536]{1,0:T(8,128)(2,1)}, bf16[128,1536]{1,0:T(8,128)(2,1)S(1)}, u32[]{:S(2)}, u32[]{:S(2)}) collective-permute-start(bf16[128,1536]{1,0:T(8,128)(2,1)} %collective-permute-done.68), channel_id=1, source_target_pairs={{0,4},{4,8},{8,12},{12,14},{14,10},{10,6},{6,2},{2,0},{1,5},{5,9},... | collective-permute-start | bytes 1179656 | tf_op jit(solution)/shard_map/ppermute | solution.py:72
  514.7 26.5 %collective-permute-start.88 = (bf16[10,64,512]{2,1,0:T(8,128)(2,1)}, bf16[10,64,512]{2,1,0:T(8,128)(2,1)S(1)}, u32[]{:S(2)}, u32[]{:S(2)}) collective-permute-start(bf16[10,64,512]{2,1,0:T(8,128)(2,1)} %collective-permute-done.87), channel_id=1, source_target_pairs={{0,4},{4,8},{8,12},{12,14},{14,10},{10,6},{6,2},{2,0},{1,5},{5,9},... | collective-permute-start | bytes 1966088 | tf_op jit(solution)/shard_map/ppermute | solution.py:72
  516.1 34.0 %collective-permute-start.95 = (bf16[10,64,512]{2,1,0:T(8,128)(2,1)}, bf16[10,64,512]{2,1,0:T(8,128)(2,1)S(1)}, u32[]{:S(2)}, u32[]{:S(2)}) collective-permute-start(bf16[10,64,512]{2,1,0:T(8,128)(2,1)} %collective-permute-done.94), channel_id=1, source_target_pairs={{0,2},{4,0},{8,4},{12,8},{14,12},{10,14},{6,10},{2,6},{1,3},{5,1},... | collective-permute-start | bytes 1966088 | tf_op jit(solution)/shard_map/ppermute | solution.py:72
  516.7 21.9 %collective-permute-start.56 = (bf16[128,512]{1,0:T(8,128)(2,1)S(1)}, bf16[128,512]{1,0:T(8,128)(2,1)S(1)}, u32[]{:S(2)}, u32[]{:S(2)}) collective-permute-start(bf16[128,512]{1,0:T(8,128)(2,1)S(1)} %collective-permute-done.55), channel_id=1, source_target_pairs={{0,4},{4,8},{8,12},{12,14},{14,10},{10,6},{6,2},{2,0},{1,5},{5,9},... | collective-permute-start | bytes 393224 | tf_op jit(solution)/shard_map/ppermute | solution.py:72
  525.8 15.5 %collective-permute-start.67 = (bf16[128,1536]{1,0:T(8,128)(2,1)S(1)}, bf16[128,1536]{1,0:T(8,128)(2,1)S(1)}, u32[]{:S(2)}, u32[]{:S(2)}) collective-permute-start(bf16[128,1536]{1,0:T(8,128)(2,1)S(1)} %collective-permute-done.66), channel_id=1, source_target_pairs={{0,2},{4,0},{8,4},{12,8},{14,12},{10,14},{6,10},{2,6},{1,3},{5,1},... | collective-permute-start | bytes 1179656 | tf_op jit(solution)/shard_map/ppermute | solution.py:72
  541.1 42.7 %collective-permute-start.48 = (bf16[8,128,1536]{2,1,0:T(8,128)(2,1)S(1)}, bf16[8,128,1536]{2,1,0:T(8,128)(2,1)S(1)}, u32[]{:S(2)}, u32[]{:S(2)}) collective-permute-start(bf16[8,128,1536]{2,1,0:T(8,128)(2,1)S(1)} %copy-done.25), channel_id=1, source_target_pairs={{0,16},{16,0},{1,17},{17,1},{2,18},{18,2},{3,19},{19,3},{4,20},{20... | collective-permute-start | bytes 9437192 | tf_op jit(solution)/shard_map/ppermute | solution.py:125
  541.3 43.1 %collective-permute-start.57 = (bf16[8,128,512]{2,1,0:T(8,128)(2,1)S(1)}, bf16[8,128,512]{2,1,0:T(8,128)(2,1)S(1)}, u32[]{:S(2)}, u32[]{:S(2)}) collective-permute-start(bf16[8,128,512]{2,1,0:T(8,128)(2,1)S(1)} %constant_dynamic-slice_fusion.2), channel_id=1, source_target_pairs={{0,16},{16,0},{1,17},{17,1},{2,18},{18,2},{3,19},{19,3},{4,20},{20... | collective-permute-start | bytes 3145736 | tf_op jit(solution)/shard_map/ppermute | solution.py:125
  547.6 12.9 %collective-permute-start.71 = (bf16[128,1536]{1,0:T(8,128)(2,1)S(1)}, bf16[128,1536]{1,0:T(8,128)(2,1)S(1)}, u32[]{:S(2)}, u32[]{:S(2)}) collective-permute-start(bf16[128,1536]{1,0:T(8,128)(2,1)S(1)} %collective-permute-done.70), channel_id=1, source_target_pairs={{0,4},{4,8},{8,12},{12,14},{14,10},{10,6},{6,2},{2,0},{1,5},{5,9},... | collective-permute-start | bytes 1179656 | tf_op jit(solution)/shard_map/ppermute | solution.py:72
  550.1 33.6 %collective-permute-start.89 = (bf16[10,64,512]{2,1,0:T(8,128)(2,1)S(1)}, bf16[10,64,512]{2,1,0:T(8,128)(2,1)S(1)}, u32[]{:S(2)}, u32[]{:S(2)}) collective-permute-start(bf16[10,64,512]{2,1,0:T(8,128)(2,1)S(1)} %collective-permute-done.88), channel_id=1, source_target_pairs={{0,4},{4,8},{8,12},{12,14},{14,10},{10,6},{6,2},{2,0},{1,5},{5,9},... | collective-permute-start | bytes 1966088 | tf_op jit(solution)/shard_map/ppermute | solution.py:72
  560.5 16.8 %collective-permute-start.96 = (bf16[10,64,512]{2,1,0:T(8,128)(2,1)S(1)}, bf16[10,64,512]{2,1,0:T(8,128)(2,1)S(1)}, u32[]{:S(2)}, u32[]{:S(2)}) collective-permute-start(bf16[10,64,512]{2,1,0:T(8,128)(2,1)S(1)} %collective-permute-done.95), channel_id=1, source_target_pairs={{0,2},{4,0},{8,4},{12,8},{14,12},{10,14},{6,10},{2,6},{1,3},{5,1},... | collective-permute-start | bytes 1966088 | tf_op jit(solution)/shard_map/ppermute | solution.py:72
  583.7 21.1 %collective-permute-start.49 = (bf16[8,128,768]{2,1,0:T(8,128)(2,1)S(1)}, bf16[8,128,768]{2,1,0:T(8,128)(2,1)S(1)}, u32[]{:S(2)}, u32[]{:S(2)}) collective-permute-start(bf16[8,128,768]{2,1,0:T(8,128)(2,1)S(1)} %constant_dynamic-slice_fusion.3), channel_id=1, source_target_pairs={{0,16},{16,0},{1,17},{17,1},{2,18},{18,2},{3,19},{19,3},{4,20},{20... | collective-permute-start | bytes 4718600 | tf_op jit(solution)/shard_map/ppermute | solution.py:125
  583.8 55.6 %collective-permute-start.73 = (bf16[8,128,1536]{2,1,0:T(8,128)(2,1)S(1)}, bf16[8,128,1536]{2,1,0:T(8,128)(2,1)}, u32[]{:S(2)}, u32[]{:S(2)}) collective-permute-start(bf16[8,128,1536]{2,1,0:T(8,128)(2,1)S(1)} %constant_dynamic-slice_fusion), channel_id=1, source_target_pairs={{0,16},{16,0},{1,17},{17,1},{2,18},{18,2},{3,19},{19,3},{4,20},{20... | collective-permute-start | bytes 9437192 | tf_op jit(solution)/shard_map/ppermute | solution.py:125
  584.4 16.7 %collective-permute-start.90 = (bf16[10,64,512]{2,1,0:T(8,128)(2,1)S(1)}, bf16[10,64,512]{2,1,0:T(8,128)(2,1)S(1)}, u32[]{:S(2)}, u32[]{:S(2)}) collective-permute-start(bf16[10,64,512]{2,1,0:T(8,128)(2,1)S(1)} %collective-permute-done.89), channel_id=1, source_target_pairs={{0,4},{4,8},{8,12},{12,14},{14,10},{10,6},{6,2},{2,0},{1,5},{5,9},... | collective-permute-start | bytes 1966088 | tf_op jit(solution)/shard_map/ppermute | solution.py:72
  588.1 14.9 %collective-permute-start.98 = (bf16[10,64,512]{2,1,0:T(8,128)(2,1)S(1)}, bf16[10,64,512]{2,1,0:T(8,128)(2,1)S(1)}, u32[]{:S(2)}, u32[]{:S(2)}) collective-permute-start(bf16[10,64,512]{2,1,0:T(8,128)(2,1)S(1)} %collective-permute-done.97), channel_id=1, source_target_pairs={{0,2},{4,0},{8,4},{12,8},{14,12},{10,14},{6,10},{2,6},{1,3},{5,1},... | collective-permute-start | bytes 1966088 | tf_op jit(solution)/shard_map/ppermute | solution.py:72
  601.1 15.9 %collective-permute-start.91 = (bf16[10,64,512]{2,1,0:T(8,128)(2,1)S(1)}, bf16[10,64,512]{2,1,0:T(8,128)(2,1)S(1)}, u32[]{:S(2)}, u32[]{:S(2)}) collective-permute-start(bf16[10,64,512]{2,1,0:T(8,128)(2,1)S(1)} %collective-permute-done.90), channel_id=1, source_target_pairs={{0,4},{4,8},{8,12},{12,14},{14,10},{10,6},{6,2},{2,0},{1,5},{5,9},... | collective-permute-start | bytes 1966088 | tf_op jit(solution)/shard_map/ppermute | solution.py:72
  603.0 14.5 %collective-permute-start.99 = (bf16[10,64,512]{2,1,0:T(8,128)(2,1)S(1)}, bf16[10,64,512]{2,1,0:T(8,128)(2,1)S(1)}, u32[]{:S(2)}, u32[]{:S(2)}) collective-permute-start(bf16[10,64,512]{2,1,0:T(8,128)(2,1)S(1)} %collective-permute-done.98), channel_id=1, source_target_pairs={{0,2},{4,0},{8,4},{12,8},{14,12},{10,14},{6,10},{2,6},{1,3},{5,1},... | collective-permute-start | bytes 1966088 | tf_op jit(solution)/shard_map/ppermute | solution.py:72
  616.9 15.0 %collective-permute-start.92 = (bf16[10,64,512]{2,1,0:T(8,128)(2,1)S(1)}, bf16[10,64,512]{2,1,0:T(8,128)(2,1)S(1)}, u32[]{:S(2)}, u32[]{:S(2)}) collective-permute-start(bf16[10,64,512]{2,1,0:T(8,128)(2,1)S(1)} %collective-permute-done.91), channel_id=1, source_target_pairs={{0,4},{4,8},{8,12},{12,14},{14,10},{10,6},{6,2},{2,0},{1,5},{5,9},... | collective-permute-start | bytes 1966088 | tf_op jit(solution)/shard_map/ppermute | solution.py:72
  (148 other events, 1628.1 us)
